TPU v7x, 128 devices: a whole 4x4x4 slice. The times are simulated.
128 devices in a mesh: box: 16 (over y, z), panel: 8 (over x, core).
Axes of the slice: x: 4, y: 4, z: 4, core: 2. Of those that a mesh axis runs over, the one named last changes fastest.
Arguments:
- field_start: float32 [4096, 4096], P('box', 'panel'), may hold values from -6 to 6
- fluid_mask: int32 [4096, 4096], P('box', 'panel'), may hold values 0 or 1
- base_visc: float32 [4096, 4096], P('box', 'panel'), may hold values from 0.02 to 0.1
- panel_cell: int32 [16384], P(('box', 'panel')), may hold values from 0 to 131071
- amplitude: bfloat16 [16384, 4096], P('box', 'panel'), may hold values from 0.049804688 to 0.5
- delay_bin: int32 [16384, 4096], P('box', 'panel'), may hold values from 0 to 2044
Outputs:
- field_end: float32 [4096, 4096], P('box', 'panel')
- signals: float32 [4096, 2048], P('panel', 'box')
Inputs may be any that keep to these rules, and one draw needn't show every extreme that they name: `panel_cell`: an index, row-major, into the 256 x 512 block of the device that owns the panel.
All inputs are finite; a program needn't handle non-finite values. No bound on the sum of `fluid_mask` on one device may be relied on, other than what follows from the above.
Results may differ from a plain program's by a relative error of at most 0.0029.
Values may be sent and summed in bfloat16 or wider, within the bound.
A program may use at most 64 MiB of HBM per device.

v0:
```python
import math

import jax
import jax.numpy as jnp
from jax import lax
from jax.sharding import PartitionSpec as P

STEPS = 4
NB = 2048


def padded(x, sides, width):
    edges = {}
    for axis, dim in sides:
        peers, length = (lax.axis_size(axis), x.shape[dim])
        up = [(i, (i + 1) % peers) for i in range(peers - 1)]
        last = lax.slice_in_dim(x, length - width, length, axis=dim)
        initial = lax.slice_in_dim(x, 0, width, axis=dim)
        edges[dim] = (
            lax.ppermute(last, axis, up),
            lax.ppermute(initial, axis, [(b, a) for a, b in up]),
        )
    done = []
    for _, dim in sides:
        low, high = edges[dim]
        around = [(width, width) if d in done else (0, 0) for d in range(x.ndim)]
        x = jnp.concatenate([jnp.pad(low, around), x, jnp.pad(high, around)], axis=dim)
        done.append(dim)
    return x


def advance(ext, mask_c, base_c):
    center = ext[1:-1, 1:-1]
    west = ext[:-2, 1:-1]
    east = ext[2:, 1:-1]
    south = ext[1:-1, :-2]
    north = ext[1:-1, 2:]
    grad_x = 0.5 * (east - west)
    grad_y = 0.5 * (north - south)
    grad_norm = jnp.sqrt(grad_x * grad_x + grad_y * grad_y)
    viscosity = base_c + 0.05 * grad_norm / (1.0 + grad_norm)
    update = center + viscosity * (east + west + north + south - 4.0 * center)
    update = update - 0.15 * (center - west) - 0.1 * (center - south)
    return mask_c * update


def signal_terms(amplitude, delay_bin, sample):
    panels, observers = amplitude.shape
    groups = NB // 128
    width = math.gcd(observers, max(1, 32768 // panels))
    blocks = observers // width
    amp_blocks = amplitude.reshape(panels, blocks, width).transpose(1, 0, 2)
    bin_blocks = delay_bin.reshape(panels, blocks, width).transpose(1, 0, 2)
    high_ids = jnp.arange(groups, dtype=jnp.int32)
    low_ids = jnp.arange(128, dtype=jnp.int32)

    def one_block(pair):
        amp_rows, bin_rows = pair
        weight = (amp_rows.astype(jnp.float32)[None, :, :] * sample[:, :, None]).astype(
            jnp.bfloat16
        )
        high = bin_rows // 128
        low = bin_rows % 128
        chosen = high[:, :, None] == high_ids[None, None, :]
        left = jnp.where(chosen[None], weight[:, :, :, None], jnp.zeros((), jnp.bfloat16))
        right = (low[:, :, None] == low_ids[None, None, :]).astype(jnp.bfloat16)
        binned = jnp.einsum("tpoh,pol->othl", left, right, preferred_element_type=jnp.float32)
        binned = binned.reshape(width, STEPS, NB)
        total = binned[:, 0, :]
        for step in range(1, STEPS):
            total = total + jnp.pad(binned[:, step, : NB - step], ((0, 0), (step, 0)))
        return total

    result = lax.map(one_block, (amp_blocks, bin_blocks))
    return result.reshape(observers, NB)


def on_device(field_start, fluid_mask, base_visc, panel_cell, amplitude, delay_bin):
    maskf = fluid_mask.astype(jnp.float32)
    taken = []
    field = field_start
    for step in range(STEPS):
        extended = padded(field, (("box", 0), ("panel", 1)), 1)
        field = advance(extended, maskf, base_visc)
        taken.append(field.reshape(-1)[panel_cell])
    sample = jnp.stack(taken)
    every = lax.all_gather(sample, ("box", "panel"), axis=1, tiled=True)
    amp_all = lax.all_to_all(amplitude, "box", split_axis=1, concat_axis=0, tiled=True)
    bin_all = lax.all_to_all(delay_bin, "box", split_axis=1, concat_axis=0, tiled=True)
    finished = signal_terms(amp_all, bin_all, every)
    signals = lax.all_to_all(finished, "box", split_axis=1, concat_axis=0, tiled=True)
    return (field, signals)


def solution(mesh):
    placed = (
        P("box", "panel"),
        P("box", "panel"),
        P("box", "panel"),
        P(("box", "panel")),
        P("box", "panel"),
        P("box", "panel"),
    )
    return jax.shard_map(
        on_device,
        mesh=mesh,
        in_specs=placed,
        out_specs=(P("box", "panel"), P("panel", "box")),
        check_vma=False,
    )
```

profile of v0, /device:TPU:1, one launch (start us, length us, event | category | flops | bytes accessed | tf_op | source)
XLA Modules:
  0.0 310.7 jit_solution(857162247917352217)
XLA Ops:
  2.8 5.0 %collective-permute-start.1 = (f32[1,512]{1,0:T(1,128)S(1)}, f32[1,512]{1,0:T(1,128)S(1)}, u32[]{:S(2)}, u32[]{:S(2)}) collective-permute-start(f32[1,512]{1,0:T(1,128)S(1)} %get-tuple-element.136), channel_id=1, source_target_pairs={{0,8},{8,16},{16,24},{24,32},{32,40},{40,48},{48,56},{56,64},{64,7... | collective-permute-start | bytes 6152 | tf_op jit(solution)/shard_map/ppermute | solution.py:20
  8.9 2.9 collective-permute-start.2
  11.7 3.1 %collective-permute-start.3 = (f32[256,1]{1,0:T(8,128)S(1)}, f32[256,1]{1,0:T(8,128)S(1)}, u32[]{:S(2)}, u32[]{:S(2)}) collective-permute-start(f32[256,1]{1,0:T(8,128)S(1)} %get-tuple-element.133), channel_id=1, source_target_pairs={{0,1},{1,2},{2,3},{3,4},{4,5},{5,6},{6,7},{8,9},{9,10},{10,11},{11... | collective-permute-start | bytes 3080 | tf_op jit(solution)/shard_map/ppermute | solution.py:20
  14.9 2.3 copy.28
  17.1 9.9 %all-to-all-start.1 = ((bf16[1024,16,32]{0,2,1:T(8,128)(2,1)}), bf16[1024,16,32]{0,2,1:T(8,128)(2,1)S(1)}, u32[]{:S(2)}, u32[]{:S(2)}) async-start(bf16[1024,16,32]{0,2,1:T(8,128)(2,1)} %bitcast.105), calls=%async_computation.1 | async-start | bytes 2097152 | tf_op jit(solution)/shard_map/all_to_all | solution.py:88
  29.2 4.0 %collective-permute-start.5 = (f32[1,512]{1,0:T(1,128)S(1)}, f32[1,512]{1,0:T(1,128)S(1)}, u32[]{:S(2)}, u32[]{:S(2)}) collective-permute-start(f32[1,512]{1,0:T(1,128)S(1)} %get-tuple-element.132), channel_id=1, source_target_pairs={{0,8},{8,16},{16,24},{24,32},{32,40},{40,48},{48,56},{56,64},{64,7... | collective-permute-start | bytes 6152 | tf_op jit(solution)/shard_map/ppermute | solution.py:20
  33.3 2.2 collective-permute-start.6
  35.5 3.4 %collective-permute-start.7 = (f32[256,1]{1,0:T(8,128)S(1)}, f32[256,1]{1,0:T(8,128)S(1)}, u32[]{:S(2)}, u32[]{:S(2)}) collective-permute-start(f32[256,1]{1,0:T(8,128)S(1)} %get-tuple-element.129), channel_id=1, source_target_pairs={{0,1},{1,2},{2,3},{3,4},{4,5},{5,6},{6,7},{8,9},{9,10},{10,11},{11... | collective-permute-start | bytes 3080 | tf_op jit(solution)/shard_map/ppermute | solution.py:20
  38.9 2.9 copy.26
  44.1 1.9 collective-permute-start.10
  46.0 3.6 %collective-permute-start.11 = (f32[256,1]{1,0:T(8,128)S(1)}, f32[256,1]{1,0:T(8,128)S(1)}, u32[]{:S(2)}, u32[]{:S(2)}) collective-permute-start(f32[256,1]{1,0:T(8,128)S(1)} %get-tuple-element.125), channel_id=1, source_target_pairs={{0,1},{1,2},{2,3},{3,4},{4,5},{5,6},{6,7},{8,9},{9,10},{10,11},{11... | collective-permute-start | bytes 3080 | tf_op jit(solution)/shard_map/ppermute | solution.py:20
  50.7 8.5 %all-to-all-start = ((s32[1024,16,32]{0,2,1:T(8,128)}), s32[1024,16,32]{0,2,1:T(8,128)S(1)}, u32[]{:S(2)}, u32[]{:S(2)}) async-start(s32[1024,16,32]{0,2,1:T(8,128)} %bitcast), calls=%async_computation | async-start | bytes 4194304 | tf_op jit(solution)/shard_map/all_to_all | solution.py:89
  61.2 4.0 %collective-permute-start.9 = (f32[1,512]{1,0:T(1,128)S(1)}, f32[1,512]{1,0:T(1,128)S(1)}, u32[]{:S(2)}, u32[]{:S(2)}) collective-permute-start(f32[1,512]{1,0:T(1,128)S(1)} %get-tuple-element.128), channel_id=1, source_target_pairs={{0,8},{8,16},{16,24},{24,32},{32,40},{40,48},{48,56},{56,64},{64,7... | collective-permute-start | bytes 6152 | tf_op jit(solution)/shard_map/ppermute | solution.py:20
  65.2 12.8 %collective-permute-done.8 = f32[1,512]{1,0:T(1,128)S(1)} collective-permute-done((f32[1,512]{1,0:T(1,128)S(1)}, f32[1,512]{1,0:T(1,128)S(1)}, u32[]{:S(2)}, u32[]{:S(2)}) %collective-permute-start.8) | collective-permute-done | bytes 2080 | tf_op jit(solution)/shard_map/ppermute | solution.py:21
  78.0 2.7 fusion.44
  81.6 1.9 collective-permute-start.14
  83.5 3.9 %collective-permute-start.15 = (f32[256,1]{1,0:T(8,128)}, f32[256,1]{1,0:T(8,128)}, u32[]{:S(2)}, u32[]{:S(2)}) collective-permute-start(f32[256,1]{1,0:T(8,128)} %get-tuple-element.121), channel_id=1, source_target_pairs={{0,1},{1,2},{2,3},{3,4},{4,5},{5,6},{6,7},{8,9},{9,10},{10,11},{11... | collective-permute-start | bytes 3080 | tf_op jit(solution)/shard_map/ppermute | solution.py:20
  89.3 4.0 %collective-permute-start.13 = (f32[1,512]{1,0:T(1,128)S(1)}, f32[1,512]{1,0:T(1,128)S(1)}, u32[]{:S(2)}, u32[]{:S(2)}) collective-permute-start(f32[1,512]{1,0:T(1,128)S(1)} %get-tuple-element.124), channel_id=1, source_target_pairs={{0,8},{8,16},{16,24},{24,32},{32,40},{40,48},{48,56},{56,64},{64,7... | collective-permute-start | bytes 6152 | tf_op jit(solution)/shard_map/ppermute | solution.py:20
  93.3 2.0 copy.36
  95.3 2.5 gather_fusion
  97.8 2.0 copy.37
  99.8 2.5 gather_fusion.1
  102.3 2.0 copy.38
  104.3 2.6 gather_fusion.2
  107.0 2.8 fusion.26
  112.6 48.2 %all_gather.3 = f32[4,16384]{1,0:T(4,128)S(1)} all-gather(f32[4,128]{1,0:T(4,128)S(1)} %pad_maximum_fusion.24), channel_id=1, replica_groups=mesh['box'=16,'panel'=8] {'box','panel'}, dimensions={1}, use_global_device_ids=true | all-gather | bytes 264192 | tf_op jit(solution)/shard_map/all_gather | solution.py:87
  160.8 2.8 copy.29
  163.6 2.6 reshape.98
  166.2 2.6 copy.27
  168.8 3.0 reshape.97
  171.8 125.7 %while.13 = (s32[]{:T(128)}, f32[16,2,2048]{2,1,0:T(2,128)S(1)}, s32[16,16384,2]{1,2,0:T(2,128)S(1)}, bf16[16,16384,2]{1,2,0:T(2,128)(2,1)}, f32[4,16384]{1,0:T(4,128)S(1)}, /*index=5*/s32[]{:T(128)}) while((s32[]{:T(128)}, f32[16,2,2048]{2,1,0:T(2,128)S(1)}, s32[16,16384,2]{1,2,0:T(2,128)S(1)}, bf16[16,16384,2]{1,2,0:T(2,128)(2,1)}, ...), condition=%wide.region_1.2_spmd.clone, body=%wide.region_0.1_spmd.clone.sunk | while | flops 544616448 | bytes 11714449 | solution.py:74
  174.5 4.9 %fusion.114 = f32[2,4,16,128]{3,2,1,0:T(8,128)S(1)} fusion(s32[16384,2]{0,1:T(2,128)S(1)} %get-tuple-element.170, bf16[4,16384,2,16]{1,3,0,2:T(8,128)(2,1)S(1)} %fusion.113), kind=kOutput, calls=%fused_computation.8.clone.3 | convolution fusion | flops 541065216 | bytes 4390912 | tf_op jit(solution)/shard_map/while/body/eval_jaxpr/tpoh,pol->othl/dot_general | solution.py:67
  182.3 4.9 %fusion.114 = f32[2,4,16,128]{3,2,1,0:T(8,128)S(1)} fusion(s32[16384,2]{0,1:T(2,128)S(1)} %get-tuple-element.170, bf16[4,16384,2,16]{1,3,0,2:T(8,128)(2,1)S(1)} %fusion.113), kind=kOutput, calls=%fused_computation.8.clone.3 | convolution fusion | flops 541065216 | bytes 4390912 | tf_op jit(solution)/shard_map/while/body/eval_jaxpr/tpoh,pol->othl/dot_general | solution.py:67
  190.2 4.9 %fusion.114 = f32[2,4,16,128]{3,2,1,0:T(8,128)S(1)} fusion(s32[16384,2]{0,1:T(2,128)S(1)} %get-tuple-element.170, bf16[4,16384,2,16]{1,3,0,2:T(8,128)(2,1)S(1)} %fusion.113), kind=kOutput, calls=%fused_computation.8.clone.3 | convolution fusion | flops 541065216 | bytes 4390912 | tf_op jit(solution)/shard_map/while/body/eval_jaxpr/tpoh,pol->othl/dot_general | solution.py:67
  198.0 4.9 %fusion.114 = f32[2,4,16,128]{3,2,1,0:T(8,128)S(1)} fusion(s32[16384,2]{0,1:T(2,128)S(1)} %get-tuple-element.170, bf16[4,16384,2,16]{1,3,0,2:T(8,128)(2,1)S(1)} %fusion.113), kind=kOutput, calls=%fused_computation.8.clone.3 | convolution fusion | flops 541065216 | bytes 4390912 | tf_op jit(solution)/shard_map/while/body/eval_jaxpr/tpoh,pol->othl/dot_general | solution.py:67
  205.9 4.9 %fusion.114 = f32[2,4,16,128]{3,2,1,0:T(8,128)S(1)} fusion(s32[16384,2]{0,1:T(2,128)S(1)} %get-tuple-element.170, bf16[4,16384,2,16]{1,3,0,2:T(8,128)(2,1)S(1)} %fusion.113), kind=kOutput, calls=%fused_computation.8.clone.3 | convolution fusion | flops 541065216 | bytes 4390912 | tf_op jit(solution)/shard_map/while/body/eval_jaxpr/tpoh,pol->othl/dot_general | solution.py:67
  213.7 4.9 %fusion.114 = f32[2,4,16,128]{3,2,1,0:T(8,128)S(1)} fusion(s32[16384,2]{0,1:T(2,128)S(1)} %get-tuple-element.170, bf16[4,16384,2,16]{1,3,0,2:T(8,128)(2,1)S(1)} %fusion.113), kind=kOutput, calls=%fused_computation.8.clone.3 | convolution fusion | flops 541065216 | bytes 4390912 | tf_op jit(solution)/shard_map/while/body/eval_jaxpr/tpoh,pol->othl/dot_general | solution.py:67
  221.6 4.9 %fusion.114 = f32[2,4,16,128]{3,2,1,0:T(8,128)S(1)} fusion(s32[16384,2]{0,1:T(2,128)S(1)} %get-tuple-element.170, bf16[4,16384,2,16]{1,3,0,2:T(8,128)(2,1)S(1)} %fusion.113), kind=kOutput, calls=%fused_computation.8.clone.3 | convolution fusion | flops 541065216 | bytes 4390912 | tf_op jit(solution)/shard_map/while/body/eval_jaxpr/tpoh,pol->othl/dot_general | solution.py:67
  229.5 4.9 %fusion.114 = f32[2,4,16,128]{3,2,1,0:T(8,128)S(1)} fusion(s32[16384,2]{0,1:T(2,128)S(1)} %get-tuple-element.170, bf16[4,16384,2,16]{1,3,0,2:T(8,128)(2,1)S(1)} %fusion.113), kind=kOutput, calls=%fused_computation.8.clone.3 | convolution fusion | flops 541065216 | bytes 4390912 | tf_op jit(solution)/shard_map/while/body/eval_jaxpr/tpoh,pol->othl/dot_general | solution.py:67
  237.3 4.9 %fusion.114 = f32[2,4,16,128]{3,2,1,0:T(8,128)S(1)} fusion(s32[16384,2]{0,1:T(2,128)S(1)} %get-tuple-element.170, bf16[4,16384,2,16]{1,3,0,2:T(8,128)(2,1)S(1)} %fusion.113), kind=kOutput, calls=%fused_computation.8.clone.3 | convolution fusion | flops 541065216 | bytes 4390912 | tf_op jit(solution)/shard_map/while/body/eval_jaxpr/tpoh,pol->othl/dot_general | solution.py:67
  245.2 4.9 %fusion.114 = f32[2,4,16,128]{3,2,1,0:T(8,128)S(1)} fusion(s32[16384,2]{0,1:T(2,128)S(1)} %get-tuple-element.170, bf16[4,16384,2,16]{1,3,0,2:T(8,128)(2,1)S(1)} %fusion.113), kind=kOutput, calls=%fused_computation.8.clone.3 | convolution fusion | flops 541065216 | bytes 4390912 | tf_op jit(solution)/shard_map/while/body/eval_jaxpr/tpoh,pol->othl/dot_general | solution.py:67
  253.0 4.9 %fusion.114 = f32[2,4,16,128]{3,2,1,0:T(8,128)S(1)} fusion(s32[16384,2]{0,1:T(2,128)S(1)} %get-tuple-element.170, bf16[4,16384,2,16]{1,3,0,2:T(8,128)(2,1)S(1)} %fusion.113), kind=kOutput, calls=%fused_computation.8.clone.3 | convolution fusion | flops 541065216 | bytes 4390912 | tf_op jit(solution)/shard_map/while/body/eval_jaxpr/tpoh,pol->othl/dot_general | solution.py:67
  260.9 4.9 %fusion.114 = f32[2,4,16,128]{3,2,1,0:T(8,128)S(1)} fusion(s32[16384,2]{0,1:T(2,128)S(1)} %get-tuple-element.170, bf16[4,16384,2,16]{1,3,0,2:T(8,128)(2,1)S(1)} %fusion.113), kind=kOutput, calls=%fused_computation.8.clone.3 | convolution fusion | flops 541065216 | bytes 4390912 | tf_op jit(solution)/shard_map/while/body/eval_jaxpr/tpoh,pol->othl/dot_general | solution.py:67
  268.7 4.9 %fusion.114 = f32[2,4,16,128]{3,2,1,0:T(8,128)S(1)} fusion(s32[16384,2]{0,1:T(2,128)S(1)} %get-tuple-element.170, bf16[4,16384,2,16]{1,3,0,2:T(8,128)(2,1)S(1)} %fusion.113), kind=kOutput, calls=%fused_computation.8.clone.3 | convolution fusion | flops 541065216 | bytes 4390912 | tf_op jit(solution)/shard_map/while/body/eval_jaxpr/tpoh,pol->othl/dot_general | solution.py:67
  276.6 4.9 %fusion.114 = f32[2,4,16,128]{3,2,1,0:T(8,128)S(1)} fusion(s32[16384,2]{0,1:T(2,128)S(1)} %get-tuple-element.170, bf16[4,16384,2,16]{1,3,0,2:T(8,128)(2,1)S(1)} %fusion.113), kind=kOutput, calls=%fused_computation.8.clone.3 | convolution fusion | flops 541065216 | bytes 4390912 | tf_op jit(solution)/shard_map/while/body/eval_jaxpr/tpoh,pol->othl/dot_general | solution.py:67
  284.5 4.9 %fusion.114 = f32[2,4,16,128]{3,2,1,0:T(8,128)S(1)} fusion(s32[16384,2]{0,1:T(2,128)S(1)} %get-tuple-element.170, bf16[4,16384,2,16]{1,3,0,2:T(8,128)(2,1)S(1)} %fusion.113), kind=kOutput, calls=%fused_computation.8.clone.3 | convolution fusion | flops 541065216 | bytes 4390912 | tf_op jit(solution)/shard_map/while/body/eval_jaxpr/tpoh,pol->othl/dot_general | solution.py:67
  292.3 4.9 %fusion.114 = f32[2,4,16,128]{3,2,1,0:T(8,128)S(1)} fusion(s32[16384,2]{0,1:T(2,128)S(1)} %get-tuple-element.170, bf16[4,16384,2,16]{1,3,0,2:T(8,128)(2,1)S(1)} %fusion.113), kind=kOutput, calls=%fused_computation.8.clone.3 | convolution fusion | flops 541065216 | bytes 4390912 | tf_op jit(solution)/shard_map/while/body/eval_jaxpr/tpoh,pol->othl/dot_general | solution.py:67
  297.9 12.2 %all_to_all.51 = f32[32,16,128]{2,0,1:T(8,128)S(1)} all-to-all(f32[32,16,128]{2,0,1:T(8,128)S(1)} %copy.30), channel_id=1, replica_groups=mesh['box'=16,'panel'=8] {'box'}, dimensions={1} | all-to-all | bytes 524288 | tf_op jit(solution)/shard_map/all_to_all | solution.py:91
  (282 shorter events, 62.8 us)
Async XLA Ops:
  0.6 26.4 %copy-start.7 = (f32[256,512]{1,0:T(8,128)S(1)}, f32[256,512]{1,0:T(8,128)}, u32[]{:S(2)}) copy-start(f32[256,512]{1,0:T(8,128)} %param.8) | copy-start | bytes 1572868
  0.6 26.4 %copy-start = (f32[256,512]{1,0:T(8,128)S(1)}, f32[256,512]{1,0:T(8,128)}, u32[]{:S(2)}) copy-start(f32[256,512]{1,0:T(8,128)} %param.10) | copy-start | bytes 1572868
  0.7 26.4 %copy-start.1 = (s32[256,512]{1,0:T(8,128)S(1)}, s32[256,512]{1,0:T(8,128)}, u32[]{:S(2)}) copy-start(s32[256,512]{1,0:T(8,128)} %param.9) | copy-start | bytes 1572868
  1.5 25.5 %collective-permute-start = (f32[1,512]{1,0:T(1,128)S(1)}, f32[1,512]{1,0:T(1,128)S(1)}, u32[]{:S(2)}, u32[]{:S(2)}) collective-permute-start(f32[1,512]{1,0:T(1,128)S(1)} %get-tuple-element.135), channel_id=1, source_target_pairs={{8,0},{16,8},{24,16},{32,24},{40,32},{48,40},{56,48},{64,56},{72,6... | collective-permute-start | bytes 6152 | tf_op jit(solution)/shard_map/ppermute | solution.py:21
  2.8 24.2 %collective-permute-start.1 = (f32[1,512]{1,0:T(1,128)S(1)}, f32[1,512]{1,0:T(1,128)S(1)}, u32[]{:S(2)}, u32[]{:S(2)}) collective-permute-start(f32[1,512]{1,0:T(1,128)S(1)} %get-tuple-element.136), channel_id=1, source_target_pairs={{0,8},{8,16},{16,24},{24,32},{32,40},{40,48},{48,56},{56,64},{64,7... | collective-permute-start | bytes 6152 | tf_op jit(solution)/shard_map/ppermute | solution.py:20
  8.9 18.1 %collective-permute-start.2 = (f32[256,1]{1,0:T(8,128)S(1)}, f32[256,1]{1,0:T(8,128)S(1)}, u32[]{:S(2)}, u32[]{:S(2)}) collective-permute-start(f32[256,1]{1,0:T(8,128)S(1)} %get-tuple-element.134), channel_id=1, source_target_pairs={{1,0},{2,1},{3,2},{4,3},{5,4},{6,5},{7,6},{9,8},{10,9},{11,10},{12... | collective-permute-start | bytes 3080 | tf_op jit(solution)/shard_map/ppermute | solution.py:21
  11.7 15.3 %collective-permute-start.3 = (f32[256,1]{1,0:T(8,128)S(1)}, f32[256,1]{1,0:T(8,128)S(1)}, u32[]{:S(2)}, u32[]{:S(2)}) collective-permute-start(f32[256,1]{1,0:T(8,128)S(1)} %get-tuple-element.133), channel_id=1, source_target_pairs={{0,1},{1,2},{2,3},{3,4},{4,5},{5,6},{6,7},{8,9},{9,10},{10,11},{11... | collective-permute-start | bytes 3080 | tf_op jit(solution)/shard_map/ppermute | solution.py:20
  17.1 32.5 %all-to-all-start.1 = ((bf16[1024,16,32]{0,2,1:T(8,128)(2,1)}), bf16[1024,16,32]{0,2,1:T(8,128)(2,1)S(1)}, u32[]{:S(2)}, u32[]{:S(2)}) async-start(bf16[1024,16,32]{0,2,1:T(8,128)(2,1)} %bitcast.105), calls=%async_computation.1 | async-start | bytes 2097152 | tf_op jit(solution)/shard_map/all_to_all | solution.py:88
  27.9 21.8 %copy-start.2 = (f32[256,512]{1,0:T(8,128)}, f32[256,512]{1,0:T(8,128)S(1)}, u32[]{:S(2)}) copy-start(f32[256,512]{1,0:T(8,128)S(1)} %fusion.80) | copy-start | bytes 1572868
  27.9 13.9 %collective-permute-start.4 = (f32[1,512]{1,0:T(1,128)S(1)}, f32[1,512]{1,0:T(1,128)S(1)}, u32[]{:S(2)}, u32[]{:S(2)}) collective-permute-start(f32[1,512]{1,0:T(1,128)S(1)} %get-tuple-element.131), channel_id=1, source_target_pairs={{8,0},{16,8},{24,16},{32,24},{40,32},{48,40},{56,48},{64,56},{72,6... | collective-permute-start | bytes 6152 | tf_op jit(solution)/shard_map/ppermute | solution.py:21
  29.2 12.6 %collective-permute-start.5 = (f32[1,512]{1,0:T(1,128)S(1)}, f32[1,512]{1,0:T(1,128)S(1)}, u32[]{:S(2)}, u32[]{:S(2)}) collective-permute-start(f32[1,512]{1,0:T(1,128)S(1)} %get-tuple-element.132), channel_id=1, source_target_pairs={{0,8},{8,16},{16,24},{24,32},{32,40},{40,48},{48,56},{56,64},{64,7... | collective-permute-start | bytes 6152 | tf_op jit(solution)/shard_map/ppermute | solution.py:20
  33.3 8.5 %collective-permute-start.6 = (f32[256,1]{1,0:T(8,128)S(1)}, f32[256,1]{1,0:T(8,128)S(1)}, u32[]{:S(2)}, u32[]{:S(2)}) collective-permute-start(f32[256,1]{1,0:T(8,128)S(1)} %get-tuple-element.130), channel_id=1, source_target_pairs={{1,0},{2,1},{3,2},{4,3},{5,4},{6,5},{7,6},{9,8},{10,9},{11,10},{12... | collective-permute-start | bytes 3080 | tf_op jit(solution)/shard_map/ppermute | solution.py:21
  35.5 6.4 %collective-permute-start.7 = (f32[256,1]{1,0:T(8,128)S(1)}, f32[256,1]{1,0:T(8,128)S(1)}, u32[]{:S(2)}, u32[]{:S(2)}) collective-permute-start(f32[256,1]{1,0:T(8,128)S(1)} %get-tuple-element.129), channel_id=1, source_target_pairs={{0,1},{1,2},{2,3},{3,4},{4,5},{5,6},{6,7},{8,9},{9,10},{10,11},{11... | collective-permute-start | bytes 3080 | tf_op jit(solution)/shard_map/ppermute | solution.py:20
  41.8 23.4 %copy-start.8 = (s32[128]{0:T(128)S(1)}, s32[128]{0:T(128)}, u32[]{:S(2)}) copy-start(s32[128]{0:T(128)} %param.11) | copy-start | bytes 1540
  42.6 0.8 copy-start.3
  44.1 21.1 %collective-permute-start.10 = (f32[256,1]{1,0:T(8,128)}, f32[256,1]{1,0:T(8,128)S(1)}, u32[]{:S(2)}, u32[]{:S(2)}) collective-permute-start(f32[256,1]{1,0:T(8,128)} %get-tuple-element.126), channel_id=1, source_target_pairs={{1,0},{2,1},{3,2},{4,3},{5,4},{6,5},{7,6},{9,8},{10,9},{11,10},{12... | collective-permute-start | bytes 3080 | tf_op jit(solution)/shard_map/ppermute | solution.py:21
  46.0 19.2 %collective-permute-start.11 = (f32[256,1]{1,0:T(8,128)S(1)}, f32[256,1]{1,0:T(8,128)S(1)}, u32[]{:S(2)}, u32[]{:S(2)}) collective-permute-start(f32[256,1]{1,0:T(8,128)S(1)} %get-tuple-element.125), channel_id=1, source_target_pairs={{0,1},{1,2},{2,3},{3,4},{4,5},{5,6},{6,7},{8,9},{9,10},{10,11},{11... | collective-permute-start | bytes 3080 | tf_op jit(solution)/shard_map/ppermute | solution.py:20
  49.7 1.0 copy-start.5
  50.7 115.6 %all-to-all-start = ((s32[1024,16,32]{0,2,1:T(8,128)}), s32[1024,16,32]{0,2,1:T(8,128)S(1)}, u32[]{:S(2)}, u32[]{:S(2)}) async-start(s32[1024,16,32]{0,2,1:T(8,128)} %bitcast), calls=%async_computation | async-start | bytes 4194304 | tf_op jit(solution)/shard_map/all_to_all | solution.py:89
  59.9 18.1 %collective-permute-start.8 = (f32[1,512]{1,0:T(1,128)S(1)}, f32[1,512]{1,0:T(1,128)S(1)}, u32[]{:S(2)}, u32[]{:S(2)}) collective-permute-start(f32[1,512]{1,0:T(1,128)S(1)} %get-tuple-element.127), channel_id=1, source_target_pairs={{8,0},{16,8},{24,16},{32,24},{40,32},{48,40},{56,48},{64,56},{72,6... | collective-permute-start | bytes 6152 | tf_op jit(solution)/shard_map/ppermute | solution.py:21
  61.2 16.8 %collective-permute-start.9 = (f32[1,512]{1,0:T(1,128)S(1)}, f32[1,512]{1,0:T(1,128)S(1)}, u32[]{:S(2)}, u32[]{:S(2)}) collective-permute-start(f32[1,512]{1,0:T(1,128)S(1)} %get-tuple-element.128), channel_id=1, source_target_pairs={{0,8},{8,16},{16,24},{24,32},{32,40},{40,48},{48,56},{56,64},{64,7... | collective-permute-start | bytes 6152 | tf_op jit(solution)/shard_map/ppermute | solution.py:20
  80.7 6.7 %copy-start.4 = (f32[256,512]{1,0:T(8,128)}, f32[256,512]{1,0:T(8,128)S(1)}, u32[]{:S(2)}) copy-start(f32[256,512]{1,0:T(8,128)S(1)} %fusion.44) | copy-start | bytes 1572868
  81.6 25.4 %collective-permute-start.14 = (f32[256,1]{1,0:T(8,128)}, f32[256,1]{1,0:T(8,128)S(1)}, u32[]{:S(2)}, u32[]{:S(2)}) collective-permute-start(f32[256,1]{1,0:T(8,128)} %get-tuple-element.122), channel_id=1, source_target_pairs={{1,0},{2,1},{3,2},{4,3},{5,4},{6,5},{7,6},{9,8},{10,9},{11,10},{12... | collective-permute-start | bytes 3080 | tf_op jit(solution)/shard_map/ppermute | solution.py:21
  83.5 23.4 %collective-permute-start.15 = (f32[256,1]{1,0:T(8,128)}, f32[256,1]{1,0:T(8,128)}, u32[]{:S(2)}, u32[]{:S(2)}) collective-permute-start(f32[256,1]{1,0:T(8,128)} %get-tuple-element.121), channel_id=1, source_target_pairs={{0,1},{1,2},{2,3},{3,4},{4,5},{5,6},{6,7},{8,9},{9,10},{10,11},{11... | collective-permute-start | bytes 3080 | tf_op jit(solution)/shard_map/ppermute | solution.py:20
  88.0 18.9 %collective-permute-start.12 = (f32[1,512]{1,0:T(1,128)}, f32[1,512]{1,0:T(1,128)S(1)}, u32[]{:S(2)}, u32[]{:S(2)}) collective-permute-start(f32[1,512]{1,0:T(1,128)} %get-tuple-element.123), channel_id=1, source_target_pairs={{8,0},{16,8},{24,16},{32,24},{40,32},{48,40},{56,48},{64,56},{72,6... | collective-permute-start | bytes 6152 | tf_op jit(solution)/shard_map/ppermute | solution.py:21
  89.3 17.6 %collective-permute-start.13 = (f32[1,512]{1,0:T(1,128)S(1)}, f32[1,512]{1,0:T(1,128)S(1)}, u32[]{:S(2)}, u32[]{:S(2)}) collective-permute-start(f32[1,512]{1,0:T(1,128)S(1)} %get-tuple-element.124), channel_id=1, source_target_pairs={{0,8},{8,16},{16,24},{24,32},{32,40},{40,48},{48,56},{56,64},{64,7... | collective-permute-start | bytes 6152 | tf_op jit(solution)/shard_map/ppermute | solution.py:20
  109.8 0.8 copy-start.6
where the time goes:
time: 313 us; the launch traced here: 311 us
  matrix products  78.2 us (25%)
  starting transfers between devices  63.4 us (20%)
  blocking collectives  60.4 us (19%)
  other arithmetic  51.4 us (16%)
  local copies, waits for them, and re-layouts  41.6 us (13%)
  waiting for transfers between devices  12.8 us (4%)
    dot_general x16, matrix products, one_block(): jnp.einsum('tpoh,pol->othl', left, right, preferred_element_type=jnp.floa...  78.2 us
    all_gather x1, blocking collectives, on_device(): every = lax.all_gather(sample, ('box', 'panel'), axis=1, tiled=True)  48.2 us
    ppermute x8, starting transfers between devices, padded(): lax.ppermute(last, axis, up)  31 us
    unnamed x25, local copies, waits for them, and re-layouts  14.5 us
    mul x16, other arithmetic, one_block(): amp_rows.astype(jnp.float32)[None, :, :] * sample[:, :, None]  14.3 us
    ppermute x8, starting transfers between devices, padded(): lax.ppermute(initial, axis, [(b, a) for a, b in up])  14 us
    dot_general x16, other arithmetic, one_block(): jnp.einsum('tpoh,pol->othl', left, right, preferred_element_type=jnp.floa...  13.6 us
    ppermute x8, waiting for transfers between devices, padded(): lax.ppermute(initial, axis, [(b, a) for a, b in up])  12.8 us
  transfers between devices with their start and end apart: 18, of which 1 were waited for; matrix products, arithmetic and copies ran while one was open for 12% of the time, Pallas kernels for 0%

commit v1 on v0

v1 whole, which is shorter than its diff:
```python
import functools

import jax
import jax.numpy as jnp
from jax import lax
from jax.experimental import pallas as pl
from jax.experimental.pallas import tpu as pltpu
from jax.sharding import PartitionSpec as P

MESH = pl.DeviceIdType.MESH
STEPS = 4
NB = 2048
BOX = 16
PAN = 8
ROWS, COLS = 256, 512
PANELS, OBS, OWN = 1024, 512, 128
TOP, FIRST, BOT, EXT_R, EXT_C = 8, 16, 272, 288, 640
RADIX, PARTS, HIGH, LOW = 26, 5, 80, 32
STACK = 4
PER = 8
KT = 256
CHUNK = 64
CHUNKS = OBS // CHUNK
PITCH = CHUNK + 8
TOPINT = 32000.0


def roll(x, shift, axis):
    return pltpu.roll(x, shift % x.shape[axis], axis)


def kernel(
    field, mask, visc, cell, amp, dly, field_out, sig_out,
    ea, eb, em, ev, ledge, redge, got_up, got_dn, mask_up, mask_dn, got_l, got_r, corner,
    samp_own, samp_all, amp_t, high_t, low_t, sb, hist, outbox, scales, inbox, inscales,
    halo_send, halo_recv, samp_send, samp_recv, bin_send, bin_recv, sc_send, sc_recv,
):
    b = lax.axis_index("box")
    p = lax.axis_index("panel")
    has_u, has_d, has_l, has_r = b > 0, b < BOX - 1, p > 0, p < PAN - 1
    diagonals = (
        (has_u & has_l, b - 1, p - 1),
        (has_u & has_r, b - 1, p + 1),
        (has_d & has_l, b + 1, p - 1),
        (has_d & has_r, b + 1, p + 1),
    )

    barrier = pltpu.get_barrier_semaphore()

    def greet(bb, pp):
        pl.semaphore_signal(barrier, inc=1, device_id=(bb, pp), device_id_type=MESH)

    for k in range(1, PAN):
        greet(b, lax.rem(p + k, PAN))
    for k in range(1, BOX):
        greet(lax.rem(b + k, BOX), p)
    expected = jnp.int32(PAN - 1 + BOX - 1)
    for there, bb, pp in diagonals:
        expected = expected + there.astype(jnp.int32)

        @pl.when(there)
        def _(bb=bb, pp=pp):
            greet(bb, pp)

    lane = lax.broadcasted_iota(jnp.int32, (ROWS, 128), 1)
    fe, ve = field[:, :128], visc[:, :128]
    me = mask[:, :128].astype(jnp.float32)
    ledge[...] = jnp.where(
        lane < 4, fe, jnp.where(lane < 8, roll(ve, 4, 1), jnp.where(lane < 12, roll(me, 8, 1), 0.0))
    )
    fe, ve = field[:, COLS - 128 :], visc[:, COLS - 128 :]
    me = mask[:, COLS - 128 :].astype(jnp.float32)
    redge[...] = jnp.where(
        lane >= 124, fe, jnp.where(lane >= 120, roll(ve, -4, 1), jnp.where(lane >= 116, roll(me, -8, 1), 0.0))
    )
    for buf in (ea, eb):
        buf[0:8, :] = jnp.zeros((8, EXT_C), jnp.float32)
        buf[EXT_R - 8 :, :] = jnp.zeros((8, EXT_C), jnp.float32)
    ea[FIRST:BOT, :COLS] = field[...]
    ev[FIRST:BOT, :COLS] = visc[...]
    em[FIRST:BOT, :COLS] = mask[...].astype(jnp.float32)

    def send(i, there, src, dst, bb, pp):
        copy = pltpu.make_async_remote_copy(
            src_ref=src, dst_ref=dst, send_sem=halo_send.at[i], recv_sem=halo_recv.at[i],
            device_id=(bb, pp), device_id_type=MESH,
        )
        return there, copy

    pl.semaphore_wait(barrier, expected)

    lo8, hi8 = pl.ds(0, 8), pl.ds(ROWS - 8, 8)
    halos = (
        (send(0, has_u, field.at[lo8], got_dn.at[0], b - 1, p), has_d),
        (send(1, has_u, visc.at[lo8], got_dn.at[1], b - 1, p), has_d),
        (send(2, has_u, mask.at[lo8], mask_dn, b - 1, p), has_d),
        (send(3, has_d, field.at[hi8], got_up.at[0], b + 1, p), has_u),
        (send(4, has_d, visc.at[hi8], got_up.at[1], b + 1, p), has_u),
        (send(5, has_d, mask.at[hi8], mask_up, b + 1, p), has_u),
        (send(6, has_l, ledge, got_r, b, p - 1), has_r),
        (send(7, has_r, redge, got_l, b, p + 1), has_l),
        (send(8, has_d & has_r, redge.at[hi8], corner.at[0], b + 1, p + 1), has_u & has_l),
        (send(9, has_d & has_l, ledge.at[hi8], corner.at[1], b + 1, p - 1), has_u & has_r),
        (send(10, has_u & has_r, redge.at[lo8], corner.at[2], b - 1, p + 1), has_d & has_l),
        (send(11, has_u & has_l, ledge.at[lo8], corner.at[3], b - 1, p - 1), has_d & has_r),
    )
    for (there, copy), _ in halos:
        pl.when(there)(copy.start)

    def blank(flag, ref):
        @pl.when(jnp.logical_not(flag))
        def _():
            ref[...] = jnp.zeros(ref.shape, ref.dtype)

    blank(has_d, got_dn)
    blank(has_d, mask_dn)
    blank(has_u, got_up)
    blank(has_u, mask_up)
    blank(has_r, got_r)
    blank(has_l, got_l)
    blank(has_u & has_l, corner.at[0])
    blank(has_u & has_r, corner.at[1])
    blank(has_d & has_l, corner.at[2])
    blank(has_d & has_r, corner.at[3])

    def turn(i, _):
        ps = pl.ds(pl.multiple_of(i * 128, 128), 128)
        for c in range(OBS // 128):
            cs = pl.ds(c * 128, 128)
            amp_t[cs, ps] = amp[ps, cs].astype(jnp.float32).T
            d = dly[ps, cs]
            low = d & 127
            r = (low * 79) >> 11
            high_t[cs, ps] = (r * 16 + (d >> 7)).astype(jnp.float32).T
            low_t[cs, ps] = (low - RADIX * r).astype(jnp.float32).T
        return 0

    lax.fori_loop(0, PANELS // 128, turn, 0)

    for (there, copy), comes in halos:
        pl.when(comes)(copy.wait_recv)

    def side(left, right, shift, lane):
        return jnp.where(
            lane < 4, roll(right, -shift, 1), jnp.where(lane >= 124, roll(left, shift, 1), 0.0)
        )

    gl, gr = got_l[...], got_r[...]
    ea[FIRST:BOT, COLS:] = side(gl, gr, 0, lane)
    ev[FIRST:BOT, COLS:] = side(gl, gr, 4, lane)
    em[FIRST:BOT, COLS:] = side(gl, gr, 8, lane)
    lane8 = lax.broadcasted_iota(jnp.int32, (8, 128), 1)
    sub8 = lax.broadcasted_iota(jnp.int32, (8, 128), 0)
    sub_w = lax.broadcasted_iota(jnp.int32, (8, COLS), 0)
    for start, keep, keep_w, got, gmask, cl, cr in (
        (TOP, sub8 >= 4, sub_w >= 4, got_up, mask_up, corner[0], corner[1]),
        (BOT, sub8 < 4, sub_w < 4, got_dn, mask_dn, corner[2], corner[3]),
    ):
        rows = pl.ds(start, 8)
        ea[rows, :COLS] = jnp.where(keep_w, got[0], 0.0)
        ev[rows, :COLS] = jnp.where(keep_w, got[1], 0.0)
        em[rows, :COLS] = jnp.where(keep_w, gmask[...].astype(jnp.float32), 0.0)
        ea[rows, COLS:] = jnp.where(keep, side(cl, cr, 0, lane8), 0.0)
        ev[rows, COLS:] = jnp.where(keep, side(cl, cr, 4, lane8), 0.0)
        em[rows, COLS:] = jnp.where(keep, side(cl, cr, 8, lane8), 0.0)

    crow = cell[...] >> 9
    ccol = cell[...] & (COLS - 1)
    pick_c = jnp.where(
        lax.broadcasted_iota(jnp.int32, (COLS, OWN), 0) == ccol, 1.0, 0.0
    ).astype(jnp.bfloat16)
    pick_r = lax.broadcasted_iota(jnp.int32, (ROWS, OWN), 0) == crow
    samp_own[...] = jnp.zeros_like(samp_own)

    for step in range(STEPS):
        src, dst = (ea, eb) if step % 2 == 0 else (eb, ea)

        def advance(i, _, src=src, dst=dst):
            at = pl.multiple_of(TOP + 16 * i, 8)
            rows = pl.ds(at, 16)
            wide = src[pl.ds(pl.multiple_of(at - 8, 8), 32), :]
            center, west, east = wide[8:24], wide[7:23], wide[9:25]
            south = roll(center, 1, 1)
            north = roll(center, -1, 1)
            grad_x = 0.5 * (east - west)
            grad_y = 0.5 * (north - south)
            grad_norm = jnp.sqrt(grad_x * grad_x + grad_y * grad_y)
            viscosity = ev[rows, :] + 0.05 * grad_norm / (1.0 + grad_norm)
            update = center + viscosity * (east + west + north + south - 4.0 * center)
            update = update - 0.15 * (center - west) - 0.1 * (center - south)
            dst[rows, :] = em[rows, :] * update
            return 0

        lax.fori_loop(0, (EXT_R - 16) // 16, advance, 0)
        now = dst[FIRST:BOT, :COLS]
        high = now.astype(jnp.bfloat16)
        rest = now - high.astype(jnp.float32)
        middle = rest.astype(jnp.bfloat16)
        last = (rest - middle.astype(jnp.float32)).astype(jnp.bfloat16)
        found = jnp.dot(high, pick_c, preferred_element_type=jnp.float32)
        found = found + jnp.dot(middle, pick_c, preferred_element_type=jnp.float32)
        found = found + jnp.dot(last, pick_c, preferred_element_type=jnp.float32)
        samp_own[step : step + 1, :] = jnp.sum(jnp.where(pick_r, found, 0.0), axis=0, keepdims=True)

    field_out[...] = ea[FIRST:BOT, :COLS]

    mine = pl.ds(pl.multiple_of(p * OWN, OWN), OWN)
    samp_all[:, mine] = samp_own[...]

    def samp_copy(k):
        to = lax.rem(p + k, PAN)
        return pltpu.make_async_remote_copy(
            src_ref=samp_own, dst_ref=samp_all.at[:, mine], send_sem=samp_send.at[k],
            recv_sem=samp_recv.at[p], device_id=(b, to), device_id_type=MESH,
        )

    def samp_arrival(k):
        frm = lax.rem(p + k, PAN)
        return pltpu.make_async_remote_copy(
            src_ref=samp_own, dst_ref=samp_all.at[:, pl.ds(pl.multiple_of(frm * OWN, OWN), OWN)],
            send_sem=samp_send.at[k], recv_sem=samp_recv.at[frm], device_id=(b, frm), device_id_type=MESH,
        )

    for k in range(1, PAN):
        samp_copy(k).start()
    for k in range(1, PAN):
        samp_arrival(k).wait_recv()
    for t in range(STEPS):
        sb[t] = jnp.broadcast_to(samp_all[t : t + 1, :], (16, PANELS)).astype(jnp.bfloat16)

    io16 = lax.broadcasted_iota(jnp.int32, (16, KT), 0).astype(jnp.float32)
    lane16 = lax.broadcasted_iota(jnp.int32, (16, 128), 1)
    sub16 = lax.broadcasted_iota(jnp.int32, (16, 128), 0)
    zero = jnp.zeros((16, KT), jnp.bfloat16)

    def bin_group(first, slot):
        acc = None
        for k in range(PANELS // KT):
            ks = pl.ds(k * KT, KT)
            ss = [sb[t, :, ks] for t in range(STEPS)]
            lhs, rhs = [], []
            for i in range(STACK):
                o = pl.ds(first + i, 1)
                hb = jnp.broadcast_to(high_t[o, ks], (16, KT)).astype(jnp.bfloat16)
                ab = jnp.broadcast_to(amp_t[o, ks], (16, KT)).astype(jnp.bfloat16)
                lb = jnp.broadcast_to(low_t[o, ks], (16, KT)).astype(jnp.bfloat16)
                for j in range(HIGH // 16):
                    lhs.append(jnp.where(hb == (io16 + 16 * j).astype(jnp.bfloat16), ab, zero))
                for j in range(LOW // 16):
                    v = zero
                    for t in range(STEPS):
                        v = jnp.where(lb == (io16 + (16 * j - t)).astype(jnp.bfloat16), ss[t], v)
                    rhs.append(v)
            part = lax.dot_general(
                jnp.concatenate(lhs, 0), jnp.concatenate(rhs, 0), (((1,), (1,)), ((), ())),
                preferred_element_type=jnp.float32,
            )
            acc = part if acc is None else acc + part
        for i in range(STACK):
            total = None
            for r in range(PARTS):
                blk = acc[i * HIGH + 16 * r : i * HIGH + 16 * r + 16, :]
                blk = jnp.where((lane16 >= LOW * i) & (lane16 < LOW * i + LOW), blk, 0.0)
                if (RADIX * r - LOW * i) % 128:
                    blk = roll(blk, RADIX * r - LOW * i, 1)
                if r == PARTS - 1:
                    over = jnp.where((lane16 < 8) & (sub16 < 15), blk, 0.0)
                    blk = jnp.where(lane16 < 8, 0.0, blk) + roll(over, 1, 0)
                total = blk if total is None else total + blk
            hist[pl.ds(slot + i, 16, stride=PITCH), :] = total

    def bin_copy(k, c):
        to = lax.rem(b + k, BOX)
        rows = pl.ds(pl.multiple_of(c * CHUNK, CHUNK), CHUNK)
        return pltpu.make_async_remote_copy(
            src_ref=outbox.at[to, rows], dst_ref=inbox.at[b, rows], send_sem=bin_send.at[k, c],
            recv_sem=bin_recv.at[b, c], device_id=(to, p), device_id_type=MESH,
        )

    def bin_arrival(k, c):
        frm = lax.rem(b + k, BOX)
        rows = pl.ds(pl.multiple_of(c * CHUNK, CHUNK), CHUNK)
        return pltpu.make_async_remote_copy(
            src_ref=outbox.at[frm, rows], dst_ref=inbox.at[frm, rows], send_sem=bin_send.at[k, c],
            recv_sem=bin_recv.at[frm, c], device_id=(frm, p), device_id_type=MESH,
        )

    def scale_copy(k):
        to = lax.rem(b + k, BOX)
        return pltpu.make_async_remote_copy(
            src_ref=scales.at[to], dst_ref=inscales.at[b], send_sem=sc_send.at[k],
            recv_sem=sc_recv.at[b], device_id=(to, p), device_id_type=MESH,
        )

    def scale_arrival(k):
        frm = lax.rem(b + k, BOX)
        return pltpu.make_async_remote_copy(
            src_ref=scales.at[frm], dst_ref=inscales.at[frm], send_sem=sc_send.at[k],
            recv_sem=sc_recv.at[frm], device_id=(frm, p), device_id_type=MESH,
        )

    def chunk(c, _):
        def some(g, _):
            for u in range(PER):
                slot = (g * PER + u) * STACK
                bin_group(c * CHUNK + slot, slot)
            return 0

        lax.fori_loop(0, CHUNK // (STACK * PER), some, 0)
        rows = pl.ds(pl.multiple_of(c * CHUNK, CHUNK), CHUNK)
        for q in range(BOX):
            x = hist[q * PITCH : q * PITCH + CHUNK, :]
            most = jnp.max(jnp.max(jnp.abs(x), axis=0, keepdims=True), axis=1, keepdims=True)
            most = jnp.maximum(jnp.broadcast_to(most, (1, 128)), 1e-30)
            y = jnp.floor(x * (TOPINT / most) + 0.5)
            outbox[q, rows, :] = y.astype(jnp.int32).astype(jnp.int16)
            scales[q, pl.ds(c, 1), :] = most * (1.0 / TOPINT)
        for k in range(1, BOX):
            bin_copy(k, c).start()
        inbox[b, rows, :] = outbox[b, rows, :]
        return 0

    lax.fori_loop(0, CHUNKS, chunk, 0)
    for k in range(1, BOX):
        scale_copy(k).start()
    inscales[b] = scales[b]

    def arrive(k, _):
        scale_arrival(k).wait_recv()
        for c in range(CHUNKS):
            bin_arrival(k, c).wait_recv()
        return 0

    lax.fori_loop(1, BOX, arrive, 0)

    def gather(c, _):
        rows = pl.ds(pl.multiple_of(c * CHUNK, CHUNK), CHUNK)
        total = None
        for s in range(BOX):
            x = inbox[s, rows, :].astype(jnp.int32).astype(jnp.float32) * inscales[s, pl.ds(c, 1), :]
            total = x if total is None else total + x
        sig_out[rows, :] = total
        return 0

    lax.fori_loop(0, CHUNKS, gather, 0)

    for (there, copy), _ in halos:
        pl.when(there)(copy.wait_send)
    for k in range(1, PAN):
        samp_copy(k).wait_send()

    def sent(k, _):
        scale_copy(k).wait_send()
        for c in range(CHUNKS):
            bin_copy(k, c).wait_send()
        return 0

    lax.fori_loop(1, BOX, sent, 0)


def on_device(field_start, fluid_mask, base_visc, panel_cell, amplitude, delay_bin):
    f32, bf16, i32 = jnp.float32, jnp.bfloat16, jnp.int32
    vmem = lambda shape, dtype=f32: pltpu.VMEM(shape, dtype)
    dma = lambda *shape: pltpu.SemaphoreType.DMA(shape)
    scratch = [
        vmem((EXT_R, EXT_C)), vmem((EXT_R, EXT_C)), vmem((EXT_R, EXT_C)), vmem((EXT_R, EXT_C)),
        vmem((ROWS, 128)), vmem((ROWS, 128)),
        vmem((2, 8, COLS)), vmem((2, 8, COLS)), vmem((8, COLS), i32), vmem((8, COLS), i32),
        vmem((ROWS, 128)), vmem((ROWS, 128)), vmem((4, 8, 128)),
        vmem((8, OWN)), vmem((8, PANELS)),
        vmem((OBS, PANELS)), vmem((OBS, PANELS)), vmem((OBS, PANELS)),
        vmem((STEPS, 16, PANELS), bf16),
        vmem((BOX * PITCH, 128)),
        vmem((BOX, OBS, 128), jnp.int16), vmem((BOX, CHUNKS, 128)),
        vmem((BOX, OBS, 128), jnp.int16), vmem((BOX, CHUNKS, 128)),
        dma(12), dma(12), dma(PAN), dma(PAN), dma(BOX, CHUNKS), dma(BOX, CHUNKS), dma(BOX), dma(BOX),
    ]
    return pl.pallas_call(
        kernel,
        out_shape=(
            jax.ShapeDtypeStruct((ROWS, COLS), f32),
            jax.ShapeDtypeStruct((OBS, NB // BOX), f32),
        ),
        in_specs=[pl.BlockSpec(memory_space=pltpu.VMEM)] * 6,
        out_specs=(pl.BlockSpec(memory_space=pltpu.VMEM),) * 2,
        scratch_shapes=scratch,
        compiler_params=pltpu.CompilerParams(
            collective_id=0, has_side_effects=True, vmem_limit_bytes=56 * 2**20
        ),
    )(field_start, fluid_mask, base_visc, panel_cell.reshape(1, OWN), amplitude, delay_bin)


def solution(mesh):
    placed = (
        P("box", "panel"),
        P("box", "panel"),
        P("box", "panel"),
        P(("box", "panel")),
        P("box", "panel"),
        P("box", "panel"),
    )
    return jax.shard_map(
        on_device,
        mesh=mesh,
        in_specs=placed,
        out_specs=(P("box", "panel"), P("panel", "box")),
        check_vma=False,
    )
```

time: 313 us -> 75.6 us (0.24)
  matrix products: 78.2 us -> 0 us
  Pallas kernels: 0 us -> 71.2 us
  starting transfers between devices: 63.4 us -> 0 us
  blocking collectives: 60.4 us -> 0 us
  other arithmetic: 51.4 us -> 0 us
  local copies, waits for them, and re-layouts: 41.6 us -> 3.54 us
  waiting for transfers between devices: 12.8 us -> 0 us
    dot_general x16 -> x0, matrix products: 78.2 us -> none  [one_block(): jnp.einsum('tpoh,pol->othl', left, right, preferred_element_type=jnp.floa...]
    pallas_call x0 -> x1, Pallas kernels: none -> 71.2 us  [on_device(): pl.pallas_call(kernel, out_shape=(jax.ShapeDtypeStruct((ROWS, COLS), f32)...]
    all_gather x1 -> x0, blocking collectives: 48.2 us -> none  [on_device(): every = lax.all_gather(sample, ('box', 'panel'), axis=1, tiled=True)]
    ppermute x16 -> x0, starting transfers between devices: 45 us -> none  [the longest x8 31 us: padded(): lax.ppermute(last, axis, up)]
    mul x20 -> x0, other arithmetic: 21.4 us -> none  [the longest x16 14.3 us: one_block(): amp_rows.astype(jnp.float32)[None, :, :] * sample[:, :, None]]
    all_to_all x2 -> x0, starting transfers between devices: 18.4 us -> none  [the longest x1 9.88 us: on_device(): lax.all_to_all(amplitude, 'box', split_axis=1, concat_axis=0, tiled=True)]
    dot_general x16 -> x0, other arithmetic: 13.6 us -> none  [one_block(): jnp.einsum('tpoh,pol->othl', left, right, preferred_element_type=jnp.floa...]
    ppermute x16 -> x0, waiting for transfers between devices: 12.8 us -> none  [the longest x8 12.8 us: padded(): lax.ppermute(initial, axis, [(b, a) for a, b in up])]
  transfers between devices with their start and end apart: 18 -> 0, of which waited for: 1 -> 0; matrix products, arithmetic and copies ran while one was open for 12% -> 0% of each run, Pallas kernels for 0% -> 0%
where the time goes in v1:
time: 75.6 us; the launch traced here: 75.4 us
  Pallas kernels  71.2 us (94%)
  local copies, waits for them, and re-layouts  3.54 us (5%)
    pallas_call x1, Pallas kernels, on_device(): pl.pallas_call(kernel, out_shape=(jax.ShapeDtypeStruct((ROWS, COLS), f32)...  71.2 us
    unnamed x2, local copies, waits for them, and re-layouts  3.54 us

profile of v1, /device:TPU:1, one launch (start us, length us, event | category | flops | bytes accessed | tf_op | source)
XLA Modules:
  0.0 75.4 jit_solution(16267491234375673586)
XLA Ops:
  0.6 71.2 %shard_map.77 = (f32[256,512]{1,0:T(8,128)}, f32[512,128]{1,0:T(8,128)}) custom-call(f32[256,512]{1,0:T(8,128)} %field.1, s32[256,512]{1,0:T(8,128)} %mask.1, f32[256,512]{1,0:T(8,128)} %visc.1, s32[1,128]{1,0:T(1,128)} %bitcast.1, bf16[1024,512]{1,0:T(8,128)(2,1)} %amp.1, s32[1024,512]{1,0:T(8,128)} %dly.1), custom_call_target="tpu_custom_call" | custom-call | tf_op jit(solution)/shard_map/pallas_call | solution.py:378
  71.8 1.9 %copy.10 = f32[256,512]{1,0:T(8,128)} copy(f32[256,512]{1,0:T(8,128)} %get-tuple-element.4) | data formatting | bytes 1048576
  73.7 1.7 %copy.11 = f32[512,128]{1,0:T(8,128)} copy(f32[512,128]{1,0:T(8,128)} %get-tuple-element.5) | data formatting | bytes 524288

commit v2 on v1

--- a/solution.py
+++ b/solution.py
@@ -14,11 +14,12 @@
 PAN = 8
 ROWS, COLS = 256, 512
 PANELS, OBS, OWN = 1024, 512, 128
-TOP, FIRST, BOT, EXT_R, EXT_C = 8, 16, 272, 288, 640
+TOP, FIRST, BOT, EXT_R, EXT_C = 8, 16, 272, 304, 640
+STRIP = 32
 RADIX, PARTS, HIGH, LOW = 26, 5, 80, 32
 STACK = 4
-PER = 8
 KT = 256
+EARLY = 3
 CHUNK = 64
 CHUNKS = OBS // CHUNK
 PITCH = CHUNK + 8
@@ -30,10 +31,10 @@
 
 
 def kernel(
-    field, mask, visc, cell, amp, dly, field_out, sig_out,
-    ea, eb, em, ev, ledge, redge, got_up, got_dn, mask_up, mask_dn, got_l, got_r, corner,
+    field_in, mask_in, visc_in, cell_in, amp_in, dly_in, field_out, sig_out,
+    mask, cell, amp, dly, ea, eb, em, ev, ledge, redge, got_up, got_dn, mask_up, mask_dn, got_l, got_r, corner,
     samp_own, samp_all, amp_t, high_t, low_t, sb, hist, outbox, scales, inbox, inscales,
-    halo_send, halo_recv, samp_send, samp_recv, bin_send, bin_recv, sc_send, sc_recv,
+    loads, store, halo_send, halo_recv, samp_send, samp_recv, bin_send, bin_recv, sc_send, sc_recv,
 ):
     b = lax.axis_index("box")
     p = lax.axis_index("panel")
@@ -45,6 +46,17 @@
         (has_d & has_r, b + 1, p + 1),
     )
 
+    own_rows, own_cols = pl.ds(FIRST, ROWS), pl.ds(0, COLS)
+    arrivals = [
+        pltpu.make_async_copy(src, dst, loads.at[i])
+        for i, (src, dst) in enumerate((
+            (field_in, ea.at[own_rows, own_cols]), (visc_in, ev.at[own_rows, own_cols]),
+            (mask_in, mask), (cell_in, cell), (amp_in, amp), (dly_in, dly),
+        ))
+    ]
+    for copy in arrivals:
+        copy.start()
+
     barrier = pltpu.get_barrier_semaphore()
 
     def greet(bb, pp):
@@ -62,66 +74,28 @@
         def _(bb=bb, pp=pp):
             greet(bb, pp)
 
+    for buf in (ea, eb, ev, em):
+        buf[0:8, :] = jnp.zeros((8, EXT_C), jnp.float32)
+        buf[BOT + 8 :, :] = jnp.zeros((EXT_R - BOT - 8, EXT_C), jnp.float32)
+    hist[...] = jnp.zeros_like(hist)
+    samp_own[...] = jnp.zeros_like(samp_own)
+    for copy in arrivals[:4]:
+        copy.wait()
+
     lane = lax.broadcasted_iota(jnp.int32, (ROWS, 128), 1)
-    fe, ve = field[:, :128], visc[:, :128]
+    fe, ve = ea[own_rows, :128], ev[own_rows, :128]
     me = mask[:, :128].astype(jnp.float32)
     ledge[...] = jnp.where(
         lane < 4, fe, jnp.where(lane < 8, roll(ve, 4, 1), jnp.where(lane < 12, roll(me, 8, 1), 0.0))
     )
-    fe, ve = field[:, COLS - 128 :], visc[:, COLS - 128 :]
+    fe, ve = ea[own_rows, COLS - 128 : COLS], ev[own_rows, COLS - 128 : COLS]
     me = mask[:, COLS - 128 :].astype(jnp.float32)
     redge[...] = jnp.where(
         lane >= 124, fe, jnp.where(lane >= 120, roll(ve, -4, 1), jnp.where(lane >= 116, roll(me, -8, 1), 0.0))
     )
-    for buf in (ea, eb):
-        buf[0:8, :] = jnp.zeros((8, EXT_C), jnp.float32)
-        buf[EXT_R - 8 :, :] = jnp.zeros((8, EXT_C), jnp.float32)
-    ea[FIRST:BOT, :COLS] = field[...]
-    ev[FIRST:BOT, :COLS] = visc[...]
-    em[FIRST:BOT, :COLS] = mask[...].astype(jnp.float32)
-
-    def send(i, there, src, dst, bb, pp):
-        copy = pltpu.make_async_remote_copy(
-            src_ref=src, dst_ref=dst, send_sem=halo_send.at[i], recv_sem=halo_recv.at[i],
-            device_id=(bb, pp), device_id_type=MESH,
-        )
-        return there, copy
-
-    pl.semaphore_wait(barrier, expected)
-
-    lo8, hi8 = pl.ds(0, 8), pl.ds(ROWS - 8, 8)
-    halos = (
-        (send(0, has_u, field.at[lo8], got_dn.at[0], b - 1, p), has_d),
-        (send(1, has_u, visc.at[lo8], got_dn.at[1], b - 1, p), has_d),
-        (send(2, has_u, mask.at[lo8], mask_dn, b - 1, p), has_d),
-        (send(3, has_d, field.at[hi8], got_up.at[0], b + 1, p), has_u),
-        (send(4, has_d, visc.at[hi8], got_up.at[1], b + 1, p), has_u),
-        (send(5, has_d, mask.at[hi8], mask_up, b + 1, p), has_u),
-        (send(6, has_l, ledge, got_r, b, p - 1), has_r),
-        (send(7, has_r, redge, got_l, b, p + 1), has_l),
-        (send(8, has_d & has_r, redge.at[hi8], corner.at[0], b + 1, p + 1), has_u & has_l),
-        (send(9, has_d & has_l, ledge.at[hi8], corner.at[1], b + 1, p - 1), has_u & has_r),
-        (send(10, has_u & has_r, redge.at[lo8], corner.at[2], b - 1, p + 1), has_d & has_l),
-        (send(11, has_u & has_l, ledge.at[lo8], corner.at[3], b - 1, p - 1), has_d & has_r),
-    )
-    for (there, copy), _ in halos:
-        pl.when(there)(copy.start)
-
-    def blank(flag, ref):
-        @pl.when(jnp.logical_not(flag))
-        def _():
-            ref[...] = jnp.zeros(ref.shape, ref.dtype)
-
-    blank(has_d, got_dn)
-    blank(has_d, mask_dn)
-    blank(has_u, got_up)
-    blank(has_u, mask_up)
-    blank(has_r, got_r)
-    blank(has_l, got_l)
-    blank(has_u & has_l, corner.at[0])
-    blank(has_u & has_r, corner.at[1])
-    blank(has_d & has_l, corner.at[2])
-    blank(has_d & has_r, corner.at[3])
+    em[own_rows, :COLS] = mask[...].astype(jnp.float32)
+    for copy in arrivals[4:]:
+        copy.wait()
 
     def turn(i, _):
         ps = pl.ds(pl.multiple_of(i * 128, 128), 128)
@@ -135,10 +109,57 @@
             low_t[cs, ps] = (low - RADIX * r).astype(jnp.float32).T
         return 0
 
-    lax.fori_loop(0, PANELS // 128, turn, 0)
+    lax.fori_loop(0, EARLY, turn, 0)
+
+    def send(i, there, src, dst, bb, pp):
+        copy = pltpu.make_async_remote_copy(
+            src_ref=src, dst_ref=dst, send_sem=halo_send.at[i], recv_sem=halo_recv.at[i],
+            device_id=(bb, pp), device_id_type=MESH,
+        )
+        return there, copy
+
+    pl.semaphore_wait(barrier, expected)
+
+    lo8, hi8 = pl.ds(0, 8), pl.ds(ROWS - 8, 8)
+    lo_own, hi_own = pl.ds(FIRST, 8), pl.ds(BOT - 8, 8)
+    halos = (
+        (send(0, has_u, ea.at[lo_own, own_cols], got_dn.at[0], b - 1, p), has_d),
+        (send(1, has_u, ev.at[lo_own, own_cols], got_dn.at[1], b - 1, p), has_d),
+        (send(2, has_u, mask.at[lo8], mask_dn, b - 1, p), has_d),
+        (send(3, has_d, ea.at[hi_own, own_cols], got_up.at[0], b + 1, p), has_u),
+        (send(4, has_d, ev.at[hi_own, own_cols], got_up.at[1], b + 1, p), has_u),
+        (send(5, has_d, mask.at[hi8], mask_up, b + 1, p), has_u),
+        (send(6, has_l, ledge, got_r, b, p - 1), has_r),
+        (send(7, has_r, redge, got_l, b, p + 1), has_l),
+        (send(8, has_d & has_r, redge.at[hi8], corner.at[0], b + 1, p + 1), has_u & has_l),
+        (send(9, has_d & has_l, ledge.at[hi8], corner.at[1], b + 1, p - 1), has_u & has_r),
+        (send(10, has_u & has_r, redge.at[lo8], corner.at[2], b - 1, p + 1), has_d & has_l),
+        (send(11, has_u & has_l, ledge.at[lo8], corner.at[3], b - 1, p - 1), has_d & has_r),
+    )
+    for (there, copy), _ in halos:
+        pl.when(there)(copy.start)
+
+    def blank(flag, ref):
+        @pl.when(jnp.logical_not(flag))
+        def _():
+            ref[...] = jnp.zeros(ref.shape, ref.dtype)
+
+    blank(has_d, got_dn)
+    blank(has_d, mask_dn)
+    blank(has_u, got_up)
+    blank(has_u, mask_up)
+    blank(has_r, got_r)
+    blank(has_l, got_l)
+    blank(has_u & has_l, corner.at[0])
+    blank(has_u & has_r, corner.at[1])
+    blank(has_d & has_l, corner.at[2])
+    blank(has_d & has_r, corner.at[3])
+
+    lax.fori_loop(EARLY, PANELS // 128, turn, 0)
 
     for (there, copy), comes in halos:
         pl.when(comes)(copy.wait_recv)
+        pl.when(there)(copy.wait_send)
 
     def side(left, right, shift, lane):
         return jnp.where(
@@ -170,16 +191,16 @@
         lax.broadcasted_iota(jnp.int32, (COLS, OWN), 0) == ccol, 1.0, 0.0
     ).astype(jnp.bfloat16)
     pick_r = lax.broadcasted_iota(jnp.int32, (ROWS, OWN), 0) == crow
-    samp_own[...] = jnp.zeros_like(samp_own)
-
     for step in range(STEPS):
         src, dst = (ea, eb) if step % 2 == 0 else (eb, ea)
 
         def advance(i, _, src=src, dst=dst):
-            at = pl.multiple_of(TOP + 16 * i, 8)
-            rows = pl.ds(at, 16)
-            wide = src[pl.ds(pl.multiple_of(at - 8, 8), 32), :]
-            center, west, east = wide[8:24], wide[7:23], wide[9:25]
+            at = pl.multiple_of(TOP + STRIP * i, 8)
+            rows = pl.ds(at, STRIP)
+            wide = src[pl.ds(pl.multiple_of(at - 8, 8), STRIP + 16), :]
+            center = wide[8 : STRIP + 8]
+            west = roll(wide, 1, 0)[8 : STRIP + 8]
+            east = roll(wide, -1, 0)[8 : STRIP + 8]
             south = roll(center, 1, 1)
             north = roll(center, -1, 1)
             grad_x = 0.5 * (east - west)
@@ -191,18 +212,14 @@
             dst[rows, :] = em[rows, :] * update
             return 0
 
-        lax.fori_loop(0, (EXT_R - 16) // 16, advance, 0)
-        now = dst[FIRST:BOT, :COLS]
-        high = now.astype(jnp.bfloat16)
-        rest = now - high.astype(jnp.float32)
-        middle = rest.astype(jnp.bfloat16)
-        last = (rest - middle.astype(jnp.float32)).astype(jnp.bfloat16)
-        found = jnp.dot(high, pick_c, preferred_element_type=jnp.float32)
-        found = found + jnp.dot(middle, pick_c, preferred_element_type=jnp.float32)
-        found = found + jnp.dot(last, pick_c, preferred_element_type=jnp.float32)
+        lax.fori_loop(0, (EXT_R - 16) // STRIP, advance, 0)
+        found = jnp.dot(
+            dst[FIRST:BOT, :COLS].astype(jnp.bfloat16), pick_c, preferred_element_type=jnp.float32
+        )
         samp_own[step : step + 1, :] = jnp.sum(jnp.where(pick_r, found, 0.0), axis=0, keepdims=True)
 
-    field_out[...] = ea[FIRST:BOT, :COLS]
+    out = pltpu.make_async_copy(ea.at[own_rows, own_cols], field_out, store)
+    out.start()
 
     mine = pl.ds(pl.multiple_of(p * OWN, OWN), OWN)
     samp_all[:, mine] = samp_own[...]
@@ -273,16 +290,15 @@
         to = lax.rem(b + k, BOX)
         rows = pl.ds(pl.multiple_of(c * CHUNK, CHUNK), CHUNK)
         return pltpu.make_async_remote_copy(
-            src_ref=outbox.at[to, rows], dst_ref=inbox.at[b, rows], send_sem=bin_send.at[k, c],
-            recv_sem=bin_recv.at[b, c], device_id=(to, p), device_id_type=MESH,
-        )
-
-    def bin_arrival(k, c):
+            src_ref=outbox.at[to, rows], dst_ref=inbox.at[b, rows], send_sem=bin_send.at[k],
+            recv_sem=bin_recv.at[b], device_id=(to, p), device_id_type=MESH,
+        )
+
+    def bin_whole(k):
         frm = lax.rem(b + k, BOX)
-        rows = pl.ds(pl.multiple_of(c * CHUNK, CHUNK), CHUNK)
-        return pltpu.make_async_remote_copy(
-            src_ref=outbox.at[frm, rows], dst_ref=inbox.at[frm, rows], send_sem=bin_send.at[k, c],
-            recv_sem=bin_recv.at[frm, c], device_id=(frm, p), device_id_type=MESH,
+        return pltpu.make_async_remote_copy(
+            src_ref=outbox.at[frm], dst_ref=inbox.at[frm], send_sem=bin_send.at[k],
+            recv_sem=bin_recv.at[frm], device_id=(frm, p), device_id_type=MESH,
         )
 
     def scale_copy(k):
@@ -299,36 +315,45 @@
             recv_sem=sc_recv.at[frm], device_id=(frm, p), device_id_type=MESH,
         )
 
-    def chunk(c, _):
-        def some(g, _):
-            for u in range(PER):
-                slot = (g * PER + u) * STACK
-                bin_group(c * CHUNK + slot, slot)
-            return 0
-
-        lax.fori_loop(0, CHUNK // (STACK * PER), some, 0)
+    def pack(c, base):
         rows = pl.ds(pl.multiple_of(c * CHUNK, CHUNK), CHUNK)
         for q in range(BOX):
-            x = hist[q * PITCH : q * PITCH + CHUNK, :]
+            x = hist[pl.ds(pl.multiple_of(base + q * PITCH, 8), CHUNK), :]
             most = jnp.max(jnp.max(jnp.abs(x), axis=0, keepdims=True), axis=1, keepdims=True)
             most = jnp.maximum(jnp.broadcast_to(most, (1, 128)), 1e-30)
             y = jnp.floor(x * (TOPINT / most) + 0.5)
             outbox[q, rows, :] = y.astype(jnp.int32).astype(jnp.int16)
             scales[q, pl.ds(c, 1), :] = most * (1.0 / TOPINT)
+
+    def post(c):
+        rows = pl.ds(pl.multiple_of(c * CHUNK, CHUNK), CHUNK)
         for k in range(1, BOX):
             bin_copy(k, c).start()
         inbox[b, rows, :] = outbox[b, rows, :]
+
+    def chunk(c, _):
+        before = jnp.maximum(c - 1, 0)
+        side = lax.rem(c, 2) * (BOX * PITCH)
+        pack(before, BOX * PITCH - side)
+        for u in range(CHUNK // STACK):
+            bin_group(c * CHUNK + u * STACK, side + u * STACK)
+
+        @pl.when(c > 0)
+        def _():
+            post(before)
+
         return 0
 
     lax.fori_loop(0, CHUNKS, chunk, 0)
+    pack(CHUNKS - 1, (CHUNKS - 1) % 2 * (BOX * PITCH))
+    post(CHUNKS - 1)
     for k in range(1, BOX):
         scale_copy(k).start()
     inscales[b] = scales[b]
 
     def arrive(k, _):
         scale_arrival(k).wait_recv()
-        for c in range(CHUNKS):
-            bin_arrival(k, c).wait_recv()
+        bin_whole(k).wait_recv()
         return 0
 
     lax.fori_loop(1, BOX, arrive, 0)
@@ -344,15 +369,13 @@
 
     lax.fori_loop(0, CHUNKS, gather, 0)
 
-    for (there, copy), _ in halos:
-        pl.when(there)(copy.wait_send)
+    out.wait()
     for k in range(1, PAN):
         samp_copy(k).wait_send()
 
     def sent(k, _):
         scale_copy(k).wait_send()
-        for c in range(CHUNKS):
-            bin_copy(k, c).wait_send()
+        bin_whole(k).wait_send()
         return 0
 
     lax.fori_loop(1, BOX, sent, 0)
@@ -363,6 +386,7 @@
     vmem = lambda shape, dtype=f32: pltpu.VMEM(shape, dtype)
     dma = lambda *shape: pltpu.SemaphoreType.DMA(shape)
     scratch = [
+        vmem((ROWS, COLS), i32), vmem((1, OWN), i32), vmem((PANELS, OBS), bf16), vmem((PANELS, OBS), i32),
         vmem((EXT_R, EXT_C)), vmem((EXT_R, EXT_C)), vmem((EXT_R, EXT_C)), vmem((EXT_R, EXT_C)),
         vmem((ROWS, 128)), vmem((ROWS, 128)),
         vmem((2, 8, COLS)), vmem((2, 8, COLS)), vmem((8, COLS), i32), vmem((8, COLS), i32),
@@ -370,10 +394,10 @@
         vmem((8, OWN)), vmem((8, PANELS)),
         vmem((OBS, PANELS)), vmem((OBS, PANELS)), vmem((OBS, PANELS)),
         vmem((STEPS, 16, PANELS), bf16),
-        vmem((BOX * PITCH, 128)),
+        vmem((2 * BOX * PITCH, 128)),
         vmem((BOX, OBS, 128), jnp.int16), vmem((BOX, CHUNKS, 128)),
         vmem((BOX, OBS, 128), jnp.int16), vmem((BOX, CHUNKS, 128)),
-        dma(12), dma(12), dma(PAN), dma(PAN), dma(BOX, CHUNKS), dma(BOX, CHUNKS), dma(BOX), dma(BOX),
+        dma(6), pltpu.SemaphoreType.DMA, dma(12), dma(12), dma(PAN), dma(PAN), dma(BOX), dma(BOX), dma(BOX), dma(BOX),
     ]
     return pl.pallas_call(
         kernel,
@@ -381,8 +405,8 @@
             jax.ShapeDtypeStruct((ROWS, COLS), f32),
             jax.ShapeDtypeStruct((OBS, NB // BOX), f32),
         ),
-        in_specs=[pl.BlockSpec(memory_space=pltpu.VMEM)] * 6,
-        out_specs=(pl.BlockSpec(memory_space=pltpu.VMEM),) * 2,
+        in_specs=[pl.BlockSpec(memory_space=pl.ANY)] * 6,
+        out_specs=(pl.BlockSpec(memory_space=pl.ANY), pl.BlockSpec(memory_space=pltpu.VMEM)),
         scratch_shapes=scratch,
         compiler_params=pltpu.CompilerParams(
             collective_id=0, has_side_effects=True, vmem_limit_bytes=56 * 2**20

time: 75.6 us -> 67 us (0.89)
  Pallas kernels: 71.2 us -> 62.6 us
    pallas_call x1, Pallas kernels: 71.2 us -> 62.6 us  [on_device(): pl.pallas_call(kernel, out_shape=(jax.ShapeDtypeStruct((ROWS, COLS), f32)...]
where the time goes in v2:
time: 67 us; the launch traced here: 66.8 us
  Pallas kernels  62.6 us (93%)
  local copies, waits for them, and re-layouts  3.54 us (5%)
    pallas_call x1, Pallas kernels, on_device(): pl.pallas_call(kernel, out_shape=(jax.ShapeDtypeStruct((ROWS, COLS), f32)...  62.6 us
    unnamed x2, local copies, waits for them, and re-layouts  3.54 us

profile of v2, /device:TPU:1, one launch (start us, length us, event | category | flops | bytes accessed | tf_op | source)
XLA Modules:
  0.0 66.8 jit_solution(10011078345036534073)
XLA Ops:
  0.6 62.6 %shard_map.77 = (f32[256,512]{1,0:T(8,128)}, f32[512,128]{1,0:T(8,128)}) custom-call(f32[256,512]{1,0:T(8,128)} %field_in.1, s32[256,512]{1,0:T(8,128)} %mask_in.1, f32[256,512]{1,0:T(8,128)} %visc_in.1, s32[1,128]{1,0:T(1,128)} %bitcast.1, bf16[1024,512]{1,0:T(8,128)(2,1)} %amp_in.1, s32[1024,512]{1,0:T(8,128)} %dly_in.1), custom_call_target="tpu_custom_call" | custom-call | tf_op jit(solution)/shard_map/pallas_call | solution.py:402
  63.2 1.9 %copy.10 = f32[256,512]{1,0:T(8,128)} copy(f32[256,512]{1,0:T(8,128)} %get-tuple-element.4) | data formatting | bytes 1048576
  65.1 1.7 %copy.11 = f32[512,128]{1,0:T(8,128)} copy(f32[512,128]{1,0:T(8,128)} %get-tuple-element.5) | data formatting | bytes 524288

commit v3 on v2

--- a/solution.py
+++ b/solution.py
@@ -15,15 +15,18 @@
 ROWS, COLS = 256, 512
 PANELS, OBS, OWN = 1024, 512, 128
 TOP, FIRST, BOT, EXT_R, EXT_C = 8, 16, 272, 304, 640
-STRIP = 32
+STRIP = 96
 RADIX, PARTS, HIGH, LOW = 26, 5, 80, 32
 STACK = 4
 KT = 256
 EARLY = 3
 CHUNK = 64
 CHUNKS = OBS // CHUNK
+HALF = CHUNK // 2
+HALVES = OBS // HALF
 PITCH = CHUNK + 8
 TOPINT = 32000.0
+ORDER = (10, 9, 11, 6, 14, 8, 2, 5, 7, 13, 15, 12, 4, 3, 1)
 
 
 def roll(x, shift, axis):
@@ -33,7 +36,7 @@
 def kernel(
     field_in, mask_in, visc_in, cell_in, amp_in, dly_in, field_out, sig_out,
     mask, cell, amp, dly, ea, eb, em, ev, ledge, redge, got_up, got_dn, mask_up, mask_dn, got_l, got_r, corner,
-    samp_own, samp_all, amp_t, high_t, low_t, sb, hist, outbox, scales, inbox, inscales,
+    samp_own, samp_all, amp_t, high_t, low_t, sb, hist, outbox, scales, scale_out, inbox, inscales, units,
     loads, store, halo_send, halo_recv, samp_send, samp_recv, bin_send, bin_recv, sc_send, sc_recv,
 ):
     b = lax.axis_index("box")
@@ -203,12 +206,12 @@
             east = roll(wide, -1, 0)[8 : STRIP + 8]
             south = roll(center, 1, 1)
             north = roll(center, -1, 1)
-            grad_x = 0.5 * (east - west)
-            grad_y = 0.5 * (north - south)
-            grad_norm = jnp.sqrt(grad_x * grad_x + grad_y * grad_y)
-            viscosity = ev[rows, :] + 0.05 * grad_norm / (1.0 + grad_norm)
-            update = center + viscosity * (east + west + north + south - 4.0 * center)
-            update = update - 0.15 * (center - west) - 0.1 * (center - south)
+            dx, dy = east - west, north - south
+            square = dx * dx + dy * dy
+            h = square * lax.rsqrt(jnp.maximum(square, 1e-30))
+            viscosity = ev[rows, :] + 0.05 * h / (2.0 + h)
+            spread = (east + west) + (north + south) - 4.0 * center
+            update = 0.75 * center + 0.15 * west + 0.1 * south + viscosity * spread
             dst[rows, :] = em[rows, :] * update
             return 0
 
@@ -286,9 +289,9 @@
                 total = blk if total is None else total + blk
             hist[pl.ds(slot + i, 16, stride=PITCH), :] = total
 
-    def bin_copy(k, c):
+    def bin_copy(k, h):
         to = lax.rem(b + k, BOX)
-        rows = pl.ds(pl.multiple_of(c * CHUNK, CHUNK), CHUNK)
+        rows = pl.ds(pl.multiple_of(h * HALF, HALF), HALF)
         return pltpu.make_async_remote_copy(
             src_ref=outbox.at[to, rows], dst_ref=inbox.at[b, rows], send_sem=bin_send.at[k],
             recv_sem=bin_recv.at[b], device_id=(to, p), device_id_type=MESH,
@@ -304,52 +307,57 @@
     def scale_copy(k):
         to = lax.rem(b + k, BOX)
         return pltpu.make_async_remote_copy(
-            src_ref=scales.at[to], dst_ref=inscales.at[b], send_sem=sc_send.at[k],
+            src_ref=scale_out.at[to], dst_ref=inscales.at[b], send_sem=sc_send.at[k],
             recv_sem=sc_recv.at[b], device_id=(to, p), device_id_type=MESH,
         )
 
     def scale_arrival(k):
         frm = lax.rem(b + k, BOX)
         return pltpu.make_async_remote_copy(
-            src_ref=scales.at[frm], dst_ref=inscales.at[frm], send_sem=sc_send.at[k],
+            src_ref=scale_out.at[frm], dst_ref=inscales.at[frm], send_sem=sc_send.at[k],
             recv_sem=sc_recv.at[frm], device_id=(frm, p), device_id_type=MESH,
         )
 
-    def pack(c, base):
-        rows = pl.ds(pl.multiple_of(c * CHUNK, CHUNK), CHUNK)
+    def pack(h, part):
+        rows = pl.ds(pl.multiple_of(h * HALF, HALF), HALF)
         for q in range(BOX):
-            x = hist[pl.ds(pl.multiple_of(base + q * PITCH, 8), CHUNK), :]
+            at = q * PITCH + part * HALF
+            x = hist[at : at + HALF, :]
             most = jnp.max(jnp.max(jnp.abs(x), axis=0, keepdims=True), axis=1, keepdims=True)
             most = jnp.maximum(jnp.broadcast_to(most, (1, 128)), 1e-30)
-            y = jnp.floor(x * (TOPINT / most) + 0.5)
+            unit = (most * (1.0 / TOPINT)).astype(jnp.bfloat16).astype(jnp.float32)
+            y = jnp.floor(x * (1.0 / unit) + 0.5)
             outbox[q, rows, :] = y.astype(jnp.int32).astype(jnp.int16)
-            scales[q, pl.ds(c, 1), :] = most * (1.0 / TOPINT)
-
-    def post(c):
-        rows = pl.ds(pl.multiple_of(c * CHUNK, CHUNK), CHUNK)
-        for k in range(1, BOX):
-            bin_copy(k, c).start()
-        inbox[b, rows, :] = outbox[b, rows, :]
+            scales[q, pl.ds(h, 1), :] = unit
+
+    def post(h):
+        for k in ORDER:
+            bin_copy(k, h).start()
 
     def chunk(c, _):
-        before = jnp.maximum(c - 1, 0)
-        side = lax.rem(c, 2) * (BOX * PITCH)
-        pack(before, BOX * PITCH - side)
-        for u in range(CHUNK // STACK):
-            bin_group(c * CHUNK + u * STACK, side + u * STACK)
+        before = jnp.maximum(2 * c - 1, 1)
+        pack(before, 1)
+        for u in range(HALF // STACK):
+            bin_group(c * CHUNK + u * STACK, u * STACK)
+        pack(2 * c, 0)
+        for u in range(HALF // STACK, CHUNK // STACK):
+            bin_group(c * CHUNK + u * STACK, u * STACK)
 
         @pl.when(c > 0)
         def _():
             post(before)
 
+        post(2 * c)
         return 0
 
     lax.fori_loop(0, CHUNKS, chunk, 0)
-    pack(CHUNKS - 1, (CHUNKS - 1) % 2 * (BOX * PITCH))
-    post(CHUNKS - 1)
-    for k in range(1, BOX):
+    pack(HALVES - 1, 1)
+    post(HALVES - 1)
+    scale_out[...] = scales[...].astype(jnp.bfloat16)
+    for k in ORDER:
         scale_copy(k).start()
-    inscales[b] = scales[b]
+    inscales[b] = scale_out[b]
+    inbox[b] = outbox[b]
 
     def arrive(k, _):
         scale_arrival(k).wait_recv()
@@ -358,16 +366,19 @@
 
     lax.fori_loop(1, BOX, arrive, 0)
 
-    def gather(c, _):
-        rows = pl.ds(pl.multiple_of(c * CHUNK, CHUNK), CHUNK)
+    for s in range(BOX):
+        units[s] = inscales[s].astype(jnp.float32)
+
+    def gather(h, _):
+        rows = pl.ds(pl.multiple_of(h * HALF, HALF), HALF)
         total = None
         for s in range(BOX):
-            x = inbox[s, rows, :].astype(jnp.int32).astype(jnp.float32) * inscales[s, pl.ds(c, 1), :]
+            x = inbox[s, rows, :].astype(jnp.int32).astype(jnp.float32) * units[s, pl.ds(h, 1), :]
             total = x if total is None else total + x
         sig_out[rows, :] = total
         return 0
 
-    lax.fori_loop(0, CHUNKS, gather, 0)
+    lax.fori_loop(0, HALVES, gather, 0)
 
     out.wait()
     for k in range(1, PAN):
@@ -379,6 +390,17 @@
         return 0
 
     lax.fori_loop(1, BOX, sent, 0)
+
+
+def hand_over(field, signals, field_out, sig_out, sems):
+    copies = (
+        pltpu.make_async_copy(field, field_out, sems.at[0]),
+        pltpu.make_async_copy(signals, sig_out, sems.at[1]),
+    )
+    for copy in copies:
+        copy.start()
+    for copy in copies:
+        copy.wait()
 
 
 def on_device(field_start, fluid_mask, base_visc, panel_cell, amplitude, delay_bin):
@@ -394,12 +416,12 @@
         vmem((8, OWN)), vmem((8, PANELS)),
         vmem((OBS, PANELS)), vmem((OBS, PANELS)), vmem((OBS, PANELS)),
         vmem((STEPS, 16, PANELS), bf16),
-        vmem((2 * BOX * PITCH, 128)),
-        vmem((BOX, OBS, 128), jnp.int16), vmem((BOX, CHUNKS, 128)),
-        vmem((BOX, OBS, 128), jnp.int16), vmem((BOX, CHUNKS, 128)),
+        vmem((BOX * PITCH, 128)),
+        vmem((BOX, OBS, 128), jnp.int16), vmem((BOX, HALVES, 128)), vmem((BOX, HALVES, 128), bf16),
+        vmem((BOX, OBS, 128), jnp.int16), vmem((BOX, HALVES, 128), bf16), vmem((BOX, HALVES, 128)),
         dma(6), pltpu.SemaphoreType.DMA, dma(12), dma(12), dma(PAN), dma(PAN), dma(BOX), dma(BOX), dma(BOX), dma(BOX),
     ]
-    return pl.pallas_call(
+    field, signals = pl.pallas_call(
         kernel,
         out_shape=(
             jax.ShapeDtypeStruct((ROWS, COLS), f32),
@@ -412,6 +434,17 @@
             collective_id=0, has_side_effects=True, vmem_limit_bytes=56 * 2**20
         ),
     )(field_start, fluid_mask, base_visc, panel_cell.reshape(1, OWN), amplitude, delay_bin)
+    return pl.pallas_call(
+        hand_over,
+        out_shape=(
+            jax.ShapeDtypeStruct((ROWS, COLS), f32),
+            jax.ShapeDtypeStruct((OBS, NB // BOX), f32),
+        ),
+        in_specs=[pl.BlockSpec(memory_space=pltpu.VMEM)] * 2,
+        out_specs=(pl.BlockSpec(memory_space=pl.ANY),) * 2,
+        scratch_shapes=[dma(2)],
+        compiler_params=pltpu.CompilerParams(vmem_limit_bytes=4 * 2**20),
+    )(field, signals)
 
 
 def solution(mesh):

time: 67 us -> 63.1 us (0.942)
  Pallas kernels: 62.6 us -> 60.3 us
  local copies, waits for them, and re-layouts: 3.54 us -> 1.98 us
    pallas_call x1, Pallas kernels: 62.6 us -> 59.4 us  [on_device(): pl.pallas_call(kernel, out_shape=(jax.ShapeDtypeStruct((ROWS, COLS), f32)...]
    unnamed x2 -> x4, local copies, waits for them, and re-layouts: 3.54 us -> 1.98 us
    pallas_call x0 -> x1, Pallas kernels: none -> 0.89 us  [on_device(): pl.pallas_call(hand_over, out_shape=(jax.ShapeDtypeStruct((ROWS, COLS), f...]
where the time goes in v3:
time: 63.1 us; the launch traced here: 62.9 us
  Pallas kernels  60.3 us (96%)
  local copies, waits for them, and re-layouts  1.98 us (3%)
  between operations  0.65 us (1%)
    pallas_call x1, Pallas kernels, on_device(): pl.pallas_call(kernel, out_shape=(jax.ShapeDtypeStruct((ROWS, COLS), f32)...  59.4 us
    unnamed x4, local copies, waits for them, and re-layouts  1.98 us

profile of v3, /device:TPU:1, one launch (start us, length us, event | category | flops | bytes accessed | tf_op | source)
XLA Modules:
  0.0 62.9 jit_solution(4688257374972358566)
XLA Ops:
  0.6 59.4 %shard_map.77 = (f32[256,512]{1,0:T(8,128)}, f32[512,128]{1,0:T(8,128)}) custom-call(f32[256,512]{1,0:T(8,128)} %field_in.1, s32[256,512]{1,0:T(8,128)} %mask_in.1, f32[256,512]{1,0:T(8,128)} %visc_in.1, s32[1,128]{1,0:T(1,128)} %bitcast.1, bf16[1024,512]{1,0:T(8,128)(2,1)} %amp_in.1, s32[1024,512]{1,0:T(8,128)} %dly_in.1), custom_call_target="tpu_custom_call" | custom-call | tf_op jit(solution)/shard_map/pallas_call | solution.py:424
  60.0 0.0 copy-start
  60.0 1.0 %copy-done = f32[256,512]{1,0:T(8,128)S(1)} copy-done((f32[256,512]{1,0:T(8,128)S(1)}, f32[256,512]{1,0:T(8,128)}, u32[]{:S(2)}) %copy-start) | copy-done | bytes 524312
  61.1 0.0 copy-start.1
  61.1 0.9 %copy-done.1 = f32[512,128]{1,0:T(8,128)S(1)} copy-done((f32[512,128]{1,0:T(8,128)S(1)}, f32[512,128]{1,0:T(8,128)}, u32[]{:S(2)}) %copy-start.1) | copy-done | bytes 262168
  62.0 0.9 %shard_map.78 = (f32[256,512]{1,0:T(8,128)}, f32[512,128]{1,0:T(8,128)}) custom-call(f32[256,512]{1,0:T(8,128)S(1)} %copy-done, f32[512,128]{1,0:T(8,128)S(1)} %copy-done.1), custom_call_target="tpu_custom_call" | custom-call | tf_op jit(solution)/shard_map/pallas_call | solution.py:437
Async XLA Ops:
  60.0 1.0 %copy-start = (f32[256,512]{1,0:T(8,128)S(1)}, f32[256,512]{1,0:T(8,128)}, u32[]{:S(2)}) copy-start(f32[256,512]{1,0:T(8,128)} %get-tuple-element.4.field) | copy-start | bytes 1572868
  61.1 0.9 %copy-start.1 = (f32[512,128]{1,0:T(8,128)S(1)}, f32[512,128]{1,0:T(8,128)}, u32[]{:S(2)}) copy-start(f32[512,128]{1,0:T(8,128)} %get-tuple-element.5.signals) | copy-start | bytes 786436

commit v4 on v3

--- a/solution.py
+++ b/solution.py
@@ -424,8 +424,8 @@
     field, signals = pl.pallas_call(
         kernel,
         out_shape=(
-            jax.ShapeDtypeStruct((ROWS, COLS), f32),
-            jax.ShapeDtypeStruct((OBS, NB // BOX), f32),
+            pltpu.VMEM((ROWS, COLS), f32),
+            pltpu.VMEM((OBS, NB // BOX), f32),
         ),
         in_specs=[pl.BlockSpec(memory_space=pl.ANY)] * 6,
         out_specs=(pl.BlockSpec(memory_space=pl.ANY), pl.BlockSpec(memory_space=pltpu.VMEM)),

time: 63.1 us -> 60.4 us (0.957)
  local copies, waits for them, and re-layouts: 1.98 us -> 0 us
  Pallas kernels: 60.3 us -> 59.6 us
    unnamed x4 -> x0, local copies, waits for them, and re-layouts: 1.98 us -> none
    pallas_call x1, Pallas kernels: 59.4 us -> 58.7 us  [on_device(): pl.pallas_call(kernel, out_shape=(pltpu.VMEM((ROWS, COLS), f32), pltpu.VM...]
where the time goes in v4:
time: 60.4 us; the launch traced here: 60.2 us
  Pallas kernels  59.6 us (99%)
  between operations  0.64 us (1%)
    pallas_call x1, Pallas kernels, on_device(): pl.pallas_call(kernel, out_shape=(pltpu.VMEM((ROWS, COLS), f32), pltpu.VM...  58.7 us

profile of v4, /device:TPU:1, one launch (start us, length us, event | category | flops | bytes accessed | tf_op | source)
XLA Modules:
  0.0 60.2 jit_solution(4509515156995066424)
XLA Ops:
  0.6 58.7 %shard_map.77 = (f32[256,512]{1,0:T(8,128)S(1)}, f32[512,128]{1,0:T(8,128)S(1)}) custom-call(f32[256,512]{1,0:T(8,128)} %field_in.1, s32[256,512]{1,0:T(8,128)} %mask_in.1, f32[256,512]{1,0:T(8,128)} %visc_in.1, s32[1,128]{1,0:T(1,128)} %bitcast.1, bf16[1024,512]{1,0:T(8,128)(2,1)} %amp_in.1, s32[1024,512]{1,0:T(8,128)} %dly_in.1), custom_call_target="tpu_custom_call" | custom-call | tf_op jit(solution)/shard_map/pallas_call | solution.py:424
  59.3 0.9 %shard_map.78 = (f32[256,512]{1,0:T(8,128)}, f32[512,128]{1,0:T(8,128)}) custom-call(f32[256,512]{1,0:T(8,128)S(1)} %get-tuple-element.4.field, f32[512,128]{1,0:T(8,128)S(1)} %get-tuple-element.5.signals), custom_call_target="tpu_custom_call" | custom-call | tf_op jit(solution)/shard_map/pallas_call | solution.py:437

commit v5 on v4

--- a/solution.py
+++ b/solution.py
@@ -11,6 +11,7 @@
 STEPS = 4
 NB = 2048
 BOX = 16
+SIDE = 4
 PAN = 8
 ROWS, COLS = 256, 512
 PANELS, OBS, OWN = 1024, 512, 128
@@ -37,7 +38,7 @@
     field_in, mask_in, visc_in, cell_in, amp_in, dly_in, field_out, sig_out,
     mask, cell, amp, dly, ea, eb, em, ev, ledge, redge, got_up, got_dn, mask_up, mask_dn, got_l, got_r, corner,
     samp_own, samp_all, amp_t, high_t, low_t, sb, hist, outbox, scales, scale_out, inbox, inscales, units,
-    loads, store, halo_send, halo_recv, samp_send, samp_recv, bin_send, bin_recv, sc_send, sc_recv,
+    entered, loads, store, halo_send, halo_recv, samp_send, samp_recv, bin_send, bin_recv, sc_send, sc_recv,
 ):
     b = lax.axis_index("box")
     p = lax.axis_index("panel")
@@ -67,10 +68,14 @@
 
     for k in range(1, PAN):
         greet(b, lax.rem(p + k, PAN))
-    for k in range(1, BOX):
-        greet(lax.rem(b + k, BOX), p)
-    expected = jnp.int32(PAN - 1 + BOX - 1)
-    for there, bb, pp in diagonals:
+    y, z = b // SIDE, lax.rem(b, SIDE)
+    row = [y * SIDE + lax.rem(z + k, SIDE) for k in range(1, SIDE)]
+    for k in range(1, SIDE):
+        greet(row[k - 1], p)
+        greet(lax.rem(y + k, SIDE) * SIDE + z, p)
+    expected = jnp.int32(PAN - 1 + 2 * (SIDE - 1))
+    turns = ((has_u & (z == 0), b - 1, p), (has_d & (z == SIDE - 1), b + 1, p))
+    for there, bb, pp in diagonals + turns:
         expected = expected + there.astype(jnp.int32)
 
         @pl.when(there)
@@ -122,6 +127,8 @@
         return there, copy
 
     pl.semaphore_wait(barrier, expected)
+    for other in row:
+        pl.semaphore_signal(entered, inc=1, device_id=(other, p), device_id_type=MESH)
 
     lo8, hi8 = pl.ds(0, 8), pl.ds(ROWS - 8, 8)
     lo_own, hi_own = pl.ds(FIRST, 8), pl.ds(BOT - 8, 8)
@@ -350,6 +357,7 @@
         post(2 * c)
         return 0
 
+    pl.semaphore_wait(entered, SIDE - 1)
     lax.fori_loop(0, CHUNKS, chunk, 0)
     pack(HALVES - 1, 1)
     post(HALVES - 1)
@@ -419,7 +427,7 @@
         vmem((BOX * PITCH, 128)),
         vmem((BOX, OBS, 128), jnp.int16), vmem((BOX, HALVES, 128)), vmem((BOX, HALVES, 128), bf16),
         vmem((BOX, OBS, 128), jnp.int16), vmem((BOX, HALVES, 128), bf16), vmem((BOX, HALVES, 128)),
-        dma(6), pltpu.SemaphoreType.DMA, dma(12), dma(12), dma(PAN), dma(PAN), dma(BOX), dma(BOX), dma(BOX), dma(BOX),
+        pltpu.SemaphoreType.REGULAR, dma(6), pltpu.SemaphoreType.DMA, dma(12), dma(12), dma(PAN), dma(PAN), dma(BOX), dma(BOX), dma(BOX), dma(BOX),
     ]
     field, signals = pl.pallas_call(
         kernel,

time: 60.4 us -> 60.4 us (level)
  no operation moved by 1% of the time
where the time goes in v5:
time: 60.4 us; the launch traced here: 60.3 us
  Pallas kernels  59.7 us (99%)
  between operations  0.64 us (1%)
    pallas_call x1, Pallas kernels, on_device(): pl.pallas_call(kernel, out_shape=(pltpu.VMEM((ROWS, COLS), f32), pltpu.VM...  58.8 us

profile of v5, /device:TPU:1, one launch (start us, length us, event | category | flops | bytes accessed | tf_op | source)
XLA Modules:
  0.0 60.3 jit_solution(10405693820199927309)
XLA Ops:
  0.6 58.8 %shard_map.77 = (f32[256,512]{1,0:T(8,128)S(1)}, f32[512,128]{1,0:T(8,128)S(1)}) custom-call(f32[256,512]{1,0:T(8,128)} %field_in.1, s32[256,512]{1,0:T(8,128)} %mask_in.1, f32[256,512]{1,0:T(8,128)} %visc_in.1, s32[1,128]{1,0:T(1,128)} %bitcast.1, bf16[1024,512]{1,0:T(8,128)(2,1)} %amp_in.1, s32[1024,512]{1,0:T(8,128)} %dly_in.1), custom_call_target="tpu_custom_call" | custom-call | tf_op jit(solution)/shard_map/pallas_call | solution.py:432
  59.4 0.9 %shard_map.78 = (f32[256,512]{1,0:T(8,128)}, f32[512,128]{1,0:T(8,128)}) custom-call(f32[256,512]{1,0:T(8,128)S(1)} %get-tuple-element.4.field, f32[512,128]{1,0:T(8,128)S(1)} %get-tuple-element.5.signals), custom_call_target="tpu_custom_call" | custom-call | tf_op jit(solution)/shard_map/pallas_call | solution.py:445

commit v6 on v5

--- a/solution.py
+++ b/solution.py
@@ -20,7 +20,6 @@
 RADIX, PARTS, HIGH, LOW = 26, 5, 80, 32
 STACK = 4
 KT = 256
-EARLY = 3
 CHUNK = 64
 CHUNKS = OBS // CHUNK
 HALF = CHUNK // 2
@@ -102,8 +101,6 @@
         lane >= 124, fe, jnp.where(lane >= 120, roll(ve, -4, 1), jnp.where(lane >= 116, roll(me, -8, 1), 0.0))
     )
     em[own_rows, :COLS] = mask[...].astype(jnp.float32)
-    for copy in arrivals[4:]:
-        copy.wait()
 
     def turn(i, _):
         ps = pl.ds(pl.multiple_of(i * 128, 128), 128)
@@ -116,8 +113,6 @@
             high_t[cs, ps] = (r * 16 + (d >> 7)).astype(jnp.float32).T
             low_t[cs, ps] = (low - RADIX * r).astype(jnp.float32).T
         return 0
-
-    lax.fori_loop(0, EARLY, turn, 0)
 
     def send(i, there, src, dst, bb, pp):
         copy = pltpu.make_async_remote_copy(
@@ -165,7 +160,9 @@
     blank(has_d & has_l, corner.at[2])
     blank(has_d & has_r, corner.at[3])
 
-    lax.fori_loop(EARLY, PANELS // 128, turn, 0)
+    for copy in arrivals[4:]:
+        copy.wait()
+    lax.fori_loop(0, PANELS // 128, turn, 0)
 
     for (there, copy), comes in halos:
         pl.when(comes)(copy.wait_recv)

time: 60.4 us -> 60.4 us (level)
  no operation moved by 1% of the time
where the time goes in v6:
time: 60.4 us; the launch traced here: 60.3 us
  Pallas kernels  59.7 us (99%)
  between operations  0.64 us (1%)
    pallas_call x1, Pallas kernels, on_device(): pl.pallas_call(kernel, out_shape=(pltpu.VMEM((ROWS, COLS), f32), pltpu.VM...  58.8 us

profile of v6, /device:TPU:1, one launch (start us, length us, event | category | flops | bytes accessed | tf_op | source)
XLA Modules:
  0.0 60.3 jit_solution(5273834773415349025)
XLA Ops:
  0.6 58.8 %shard_map.77 = (f32[256,512]{1,0:T(8,128)S(1)}, f32[512,128]{1,0:T(8,128)S(1)}) custom-call(f32[256,512]{1,0:T(8,128)} %field_in.1, s32[256,512]{1,0:T(8,128)} %mask_in.1, f32[256,512]{1,0:T(8,128)} %visc_in.1, s32[1,128]{1,0:T(1,128)} %bitcast.1, bf16[1024,512]{1,0:T(8,128)(2,1)} %amp_in.1, s32[1024,512]{1,0:T(8,128)} %dly_in.1), custom_call_target="tpu_custom_call" | custom-call | tf_op jit(solution)/shard_map/pallas_call | solution.py:429
  59.4 0.9 %shard_map.78 = (f32[256,512]{1,0:T(8,128)}, f32[512,128]{1,0:T(8,128)}) custom-call(f32[256,512]{1,0:T(8,128)S(1)} %get-tuple-element.4.field, f32[512,128]{1,0:T(8,128)S(1)} %get-tuple-element.5.signals), custom_call_target="tpu_custom_call" | custom-call | tf_op jit(solution)/shard_map/pallas_call | solution.py:442
